TPU v7x, 8 devices: a whole 2x2x1 slice. The times are simulated.
8 devices in a mesh: rep: 2 (over y, z), dp: 4 (over x, core).
Axes of the slice: x: 2, y: 2, z: 1, core: 2. Of those that a mesh axis runs over, the one named last changes fastest.
Arguments:
- x: bfloat16 [8, 2048, 512], P(('rep', 'dp')), parts along dimension 0
- dy: bfloat16 [8, 2048, 512], P(('rep', 'dp')), parts along dimension 0
- w_gate: bfloat16 [2, 512, 8192], replicated
- w_up: bfloat16 [2, 512, 8192], replicated
- w_down: bfloat16 [2, 8192, 512], replicated
- m_w_gate: float32 [2, 512, 8192], P(None, 'dp')
- m_w_up: float32 [2, 512, 8192], P(None, 'dp')
- m_w_down: float32 [2, 8192, 512], P(None, 'dp')
- v_w_gate: float32 [2, 512, 8192], P(None, 'dp')
- v_w_up: float32 [2, 512, 8192], P(None, 'dp')
- v_w_down: float32 [2, 8192, 512], P(None, 'dp')
Outputs:
- output 1: bfloat16 [4, 512, 8192], P('rep'), parts along dimension 0
- output 2: bfloat16 [4, 512, 8192], P('rep'), parts along dimension 0
- output 3: bfloat16 [4, 8192, 512], P('rep'), parts along dimension 0
- output 4: float32 [4, 512, 8192], P('rep', 'dp'), parts along dimension 0
- output 5: float32 [4, 512, 8192], P('rep', 'dp'), parts along dimension 0
- output 6: float32 [4, 8192, 512], P('rep', 'dp'), parts along dimension 0
- output 7: float32 [4, 512, 8192], P('rep', 'dp'), parts along dimension 0
- output 8: float32 [4, 512, 8192], P('rep', 'dp'), parts along dimension 0
- output 9: float32 [4, 8192, 512], P('rep', 'dp'), parts along dimension 0
There are 2 independent parts. A program takes and returns all parts, laid end to end along the dimension named above; an argument that names none is the same for every part.
All inputs are finite; a program needn't handle non-finite values.
Results may differ from a plain program's by a relative error of at most 0.022.
Values are sent between devices in bfloat16 or wider.
A program may use at most 2 GiB of HBM per device.

v0:
```python
import jax
import jax.numpy as jnp
from jax import lax
from jax.experimental import pallas as pl
from jax.experimental.pallas import tpu as pltpu
from jax.sharding import PartitionSpec as P


F32, BF16 = jnp.float32, jnp.bfloat16
TOKENS, D, FF = 2048, 512, 8192
LAYERS, DP = 2, 4
OWN = FF // DP
SIZE = 256
PARTS = OWN // SIZE
STEPS = LAYERS * PARTS * DP
SLOTS = 3
CHUNKS = [(1, start, 512) for start in range(0, OWN, 512)] + [(0, 0, 512), (0, 512, 512), (0, 1024, 512), (0, 1536, 256), (0, 1792, 256)]
LAST = len(CHUNKS) - 1
ROWS = D // DP
COUNT = 3 * LAYERS * D * FF
VMEM = 60 * 1024 * 1024


def dot(a, b):
    return jnp.dot(a, b, preferred_element_type=F32)


def dot_nt(a, b):
    return lax.dot_general(a, b, (((1,), (1,)), ((), ())), preferred_element_type=F32)


def sigmoid(x):
    return 0.5 * jnp.tanh(0.5 * x) + 0.5


def normed(h):
    wide = h.astype(F32)
    return (wide * lax.rsqrt(jnp.mean(wide * wide, -1, keepdims=True) + 1e-6)).astype(BF16)


def flipped(t):
    return t.astype(F32).T.astype(BF16)


def whole(shape):
    return pl.BlockSpec(shape, lambda *_: (0,) * len(shape), pipeline_mode=pl.Buffered(1))


def params(n):
    return pltpu.CompilerParams(dimension_semantics=("arbitrary",) * n, vmem_limit_bytes=VMEM)


def cost(units, moved):
    return pl.CostEstimate(flops=int(units * 2 * TOKENS * D * FF), bytes_accessed=int(moved), transcendentals=0)


FT, FI = 1024, 2048


def forward_kernel(x_ref, dy_ref, wg_ref, wu_ref, wd_ref, h1_ref, a0_ref, a1_ref, a0t_ref, a1t_ref, dyt_ref, acc_ref, z_ref):
    j, i = pl.program_id(0), pl.program_id(1)
    rows = pl.ds(pl.multiple_of(i * FI, FI), FI)

    @pl.when(j == 0)
    def _():
        a = normed(x_ref[rows, :])
        a0_ref[rows, :] = a
        a0t_ref[:, rows] = flipped(a)
        dyt_ref[:, rows] = flipped(dy_ref[rows, :])
        acc_ref[rows, :] = jnp.zeros((FI, D), F32)

    a = a0_ref[rows, :]
    for s in range(0, FT, 256):
        gate = dot(a, wg_ref[0, :, s : s + 256])
        up = dot(a, wu_ref[0, :, s : s + 256])
        z_ref[:, s : s + 256] = (gate * sigmoid(gate) * up).astype(BF16)
    acc_ref[rows, :] += dot(z_ref[...], wd_ref[0])

    @pl.when(j == FF // FT - 1)
    def _():
        h1 = x_ref[rows, :] + acc_ref[rows, :].astype(BF16)
        a1 = normed(h1)
        h1_ref[rows, :] = h1
        a1_ref[rows, :] = a1
        a1t_ref[:, rows] = flipped(a1)


def forward(x, dy, wg, wu, wd):
    row, col = jax.ShapeDtypeStruct((TOKENS, D), BF16), jax.ShapeDtypeStruct((D, TOKENS), BF16)
    return pl.pallas_call(
        forward_kernel,
        grid=(FF // FT, TOKENS // FI),
        in_specs=[
            whole((TOKENS, D)),
            whole((TOKENS, D)),
            pl.BlockSpec((1, D, FT), lambda j, i: (0, 0, j)),
            pl.BlockSpec((1, D, FT), lambda j, i: (0, 0, j)),
            pl.BlockSpec((1, FT, D), lambda j, i: (0, j, 0)),
        ],
        out_specs=[whole((TOKENS, D))] * 3 + [whole((D, TOKENS))] * 3,
        out_shape=[row] * 3 + [col] * 3,
        scratch_shapes=[pltpu.VMEM((TOKENS, D), F32), pltpu.VMEM((FI, FT), BF16)],
        compiler_params=params(2),
        cost_estimate=cost(3, 40e6),
        name="forward0",
    )(x, dy, wg, wu, wd)


BI = 512


def backward_kernel(
    h1, a0, a0t, a1, a1t, dy0, dy0t, wg, wu, wd, gu_out, d_out, squares,
    a, at, dy, dyt, h, da, wgu_buf, wd_buf, z, dgu, dt, grads,
    own_gu, far_gu, give_gu, core_gu, x_gu, own_d, far_d, give_d, core_d, x_d,
    w_sem, in_sem, core_send, core_recv, x_send, x_recv, out_sem, core_free, x_free,
):
    t = pl.program_id(0)
    part, r = lax.div(t, DP), lax.rem(t, DP)
    slot = lax.rem(part, SLOTS)
    rep, me = lax.axis_index("rep"), lax.axis_index("dp")
    mx, mc = lax.div(me, 2), lax.rem(me, 2)

    def related(qx, qc):
        return lax.rem(mx + qx, 2) * 2 + lax.rem(mc + qc, 2)

    core_peer, x_peer = (rep, related(0, 1)), (rep, related(1, 0))
    mesh_id = pl.DeviceIdType.MESH

    def weights(t):
        part, r = lax.div(t, DP), lax.rem(t, DP)
        layer = 1 - lax.div(part, PARTS)
        at_ff = pl.multiple_of(related(lax.div(r, 2), lax.rem(r, 2)) * OWN + lax.rem(part, PARTS) * SIZE, SIZE)
        n = lax.rem(t, 2)
        return (
            pltpu.make_async_copy(wg.at[layer, :, pl.ds(at_ff, SIZE)], wgu_buf.at[n, :, 0:SIZE], w_sem.at[n, 0]),
            pltpu.make_async_copy(wu.at[layer, :, pl.ds(at_ff, SIZE)], wgu_buf.at[n, :, SIZE : 2 * SIZE], w_sem.at[n, 1]),
            pltpu.make_async_copy(wd.at[layer, pl.ds(at_ff, SIZE), :], wd_buf.at[n], w_sem.at[n, 2]),
        )

    def inputs(*sources):
        pairs = zip(sources, (a, at, dy, dyt, h))
        return [pltpu.make_async_copy(src, dst, in_sem.at[n]) for n, (src, dst) in enumerate(pairs)]

    def to_core(n):
        return [
            pltpu.make_async_remote_copy(src.at[n], dst.at[n], core_send.at[n, i], core_recv.at[n, i], device_id=core_peer, device_id_type=mesh_id)
            for i, (src, dst) in enumerate(((give_gu, core_gu), (give_d, core_d)))
        ]

    def to_x(n):
        return [
            pltpu.make_async_remote_copy(src.at[n], dst.at[n], x_send.at[n, i], x_recv.at[n, i], device_id=x_peer, device_id_type=mesh_id)
            for i, (src, dst) in enumerate(((far_gu, x_gu), (far_d, x_d)))
        ]

    def out(p, n):
        return [
            pltpu.make_async_copy(src.at[n], dst.at[p], out_sem.at[n, i]) for i, (src, dst) in enumerate(((own_gu, gu_out), (own_d, d_out)))
        ]

    def give(p):
        n = lax.rem(p, SLOTS)

        @pl.when(p >= SLOTS)
        def _():
            pl.semaphore_wait(core_free, 1)

        for copy in to_core(n):
            copy.start()

    def pair(p):
        n = lax.rem(p, SLOTS)
        for copy in to_core(n):
            copy.wait_recv()
        far_gu[n] = (far_gu[n].astype(F32) + core_gu[n, 1].astype(F32)).astype(BF16)
        far_d[n] = (far_d[n].astype(F32) + core_d[n, 1].astype(F32)).astype(BF16)

        @pl.when(p >= SLOTS)
        def _():
            pl.semaphore_wait(x_free, 1)

        for copy in to_x(n):
            copy.start()

    def finish(p):
        n = lax.rem(p, SLOTS)
        for copy in to_x(n):
            copy.wait()
        for copy in to_core(n):
            copy.wait_send()
        total = (own_gu[n].astype(F32) + core_gu[n, 0].astype(F32) + x_gu[n].astype(F32)).astype(BF16)
        own_gu[n] = total
        total = total.astype(F32)
        line = jnp.sum(total[0] * total[0] + total[1] * total[1], 0, keepdims=True)
        line = sum(line[:, i : i + D] for i in range(0, line.shape[1], D))
        total = (own_d[n].astype(F32) + core_d[n, 0].astype(F32) + x_d[n].astype(F32)).astype(BF16)
        own_d[n] = total
        total = total.astype(F32)
        squares[...] += line + jnp.sum(total * total, 0, keepdims=True)

        @pl.when(p < LAYERS * PARTS - SLOTS)
        def _():
            pl.semaphore_signal(core_free, inc=1, device_id=core_peer, device_id_type=mesh_id)
            pl.semaphore_signal(x_free, inc=1, device_id=x_peer, device_id_type=mesh_id)

        for copy in out(p, n):
            copy.start()

    @pl.when(t == 0)
    def _():
        barrier = pltpu.get_barrier_semaphore()
        for peer in (core_peer, x_peer):
            pl.semaphore_signal(barrier, inc=1, device_id=peer, device_id_type=mesh_id)
        for copy in (*weights(t), *inputs(a1, a1t, dy0, dy0t, h1)):
            copy.start()
        da[...] = jnp.zeros_like(da)
        squares[...] = jnp.zeros_like(squares)
        for copy in inputs(a1, a1t, dy0, dy0t, h1):
            copy.wait()
        pl.semaphore_wait(barrier, 2)

    for copy in weights(t):
        copy.wait()

    @pl.when(t < STEPS - 1)
    def _():
        for copy in weights(t + 1):
            copy.start()

    @pl.when(t == STEPS // 2)
    def _():
        for copy in inputs(a0, a0t):
            copy.start()
        for b in range(0, TOKENS, BI):
            rows = slice(b, b + BI)
            back = da[rows, :].astype(BF16).astype(F32)
            wide = h[rows, :].astype(F32)
            scale = lax.rsqrt(jnp.mean(wide * wide, -1, keepdims=True) + 1e-6)
            along = jnp.mean(back * wide, -1, keepdims=True)
            dh = dy[rows, :] + (back * scale - wide * (scale * scale * scale * along)).astype(BF16)
            dy[rows, :] = dh
            dyt[:, rows] = flipped(dh)
        for copy in inputs(a0, a0t):
            copy.wait()

    def tile(with_da):
        w = lax.rem(t, 2)
        for b in range(0, TOKENS, BI):
            rows = slice(b, b + BI)
            both = dot(a[rows, :], wgu_buf[w])
            gate, up = both[:, :SIZE], both[:, SIZE:]
            dz = dot_nt(dy[rows, :], wd_buf[w]).astype(BF16).astype(F32)
            sig = sigmoid(gate)
            act = gate * sig
            z[rows, :] = (act * up).astype(BF16)
            dgu[rows, SIZE : 2 * SIZE] = (dz * act).astype(BF16)
            dgu[rows, 0:SIZE] = (dz * up * (sig + act * (1.0 - sig))).astype(BF16)
        dt[...] = dot(dyt[...], z[...]).T.astype(BF16)
        grads[...] = dot(at[...], dgu[...]).astype(BF16)
        if with_da:
            for b in range(0, TOKENS, BI):
                rows = slice(b, b + BI)
                da[rows, :] += dot_nt(dgu[rows, :], wgu_buf[w])

    @pl.when(t < STEPS // 2)
    def _():
        tile(True)

    @pl.when(t >= STEPS // 2)
    def _():
        tile(False)

    columns = pl.ds(pl.multiple_of(related(lax.div(r, 2), lax.rem(r, 2)) * SIZE, SIZE), SIZE)
    for q, (gu, d) in enumerate(((own_gu, own_d), (give_gu.at[:, 0], give_d.at[:, 0]), (far_gu, far_d), (give_gu.at[:, 1], give_d.at[:, 1]))):
        rows = pl.ds(pl.multiple_of(related(q // 2, q % 2) * ROWS, ROWS), ROWS)
        for i in range(2):
            gu[slot, i, :, columns] = grads[rows, i * SIZE : (i + 1) * SIZE]

        @pl.when(r == q)
        def _(d=d):
            d[slot] = dt[...]

    @pl.when((r == 0) & (part >= 1))
    def _():
        pair(part - 1)

    @pl.when((r == 2) & (part >= 2))
    def _():
        finish(part - 2)

    @pl.when((r == 3) & (part >= 2))
    def _():
        for copy in out(part - 2, lax.rem(part - 2, SLOTS)):
            copy.wait()

    @pl.when(r == 3)
    def _():
        give(part)

    @pl.when(t == STEPS - 1)
    def _():
        pair(part)
        finish(part - 1)
        finish(part)
        for p in (part - 1, part):
            for copy in out(p, lax.rem(p, SLOTS)):
                copy.wait()


def backward(h1, a0, a0t, a1, a1t, dy, dyt, wg, wu, wd):
    wide = DP * SIZE
    row, col, vm, dma = (TOKENS, D), (D, TOKENS), pltpu.VMEM, pltpu.SemaphoreType.DMA
    gu, d = (SLOTS, 2, ROWS, wide), (SLOTS, SIZE, D)
    two_gu, two_d = (SLOTS, 2, 2, ROWS, wide), (SLOTS, 2, SIZE, D)
    return pl.pallas_call(
        backward_kernel,
        grid=(STEPS,),
        in_specs=[pl.BlockSpec(memory_space=pl.ANY)] * 10,
        out_specs=[pl.BlockSpec(memory_space=pl.ANY)] * 2 + [pl.BlockSpec((1, D), lambda t: (0, 0))],
        out_shape=[
            jax.ShapeDtypeStruct((LAYERS * PARTS, 2, ROWS, wide), BF16),
            jax.ShapeDtypeStruct((LAYERS * PARTS, SIZE, D), BF16),
            jax.ShapeDtypeStruct((1, D), F32),
        ],
        scratch_shapes=[
            *(vm(shape, BF16) for shape in (row, col, row, col, row)),
            vm(row, F32),
            *(vm(shape, BF16) for shape in ((2, D, 2 * SIZE), (2, SIZE, D), (TOKENS, SIZE), (TOKENS, 2 * SIZE), (SIZE, D), (D, 2 * SIZE))),
            *(vm(shape, BF16) for shape in (gu, gu, two_gu, two_gu, gu, d, d, two_d, two_d, d)),
            dma((2, 3)),
            dma((5,)),
            *[dma((SLOTS, 2))] * 5,
            pltpu.SemaphoreType.REGULAR,
            pltpu.SemaphoreType.REGULAR,
        ],
        compiler_params=pltpu.CompilerParams(
            dimension_semantics=("arbitrary",), vmem_limit_bytes=VMEM, collective_id=0, has_side_effects=True
        ),
        cost_estimate=cost(14, 120e6),
        name="backward",
    )(h1, a0, a0t, a1, a1t, dy, dyt, wg, wu, wd)


def adamw_kernel(me_ref, f_ref, ggu, gd, wg, wu, wd, mg, mu, md, vg, vu, vd, *refs):
    ngu, nd, *mv = refs[-8:]
    factor = f_ref[0, 0]
    for k, (g, w, m, v, to) in enumerate(
        (
            (jnp.concatenate([ggu[p, 0] for p in range(ggu.shape[0])], 1), wg.at[0], mg.at[0], vg.at[0], ngu.at[0]),
            (jnp.concatenate([ggu[p, 1] for p in range(ggu.shape[0])], 1), wu.at[0], mu.at[0], vu.at[0], ngu.at[1]),
            (gd[...], wd.at[0], md.at[0], vd.at[0], nd),
        )
    ):
        g = g.astype(F32) * factor
        m = 0.9 * m[...] + 0.1 * g
        v = 0.95 * v[...] + 0.05 * g * g
        w = w[...].astype(F32)
        to[...] = (w - 0.02 * (m * lax.rsqrt(v + 1e-8) + 0.1 * w)).astype(BF16)
        mv[k][0] = m
        mv[3 + k][0] = v


def adamw(chunk, me, factor, ggu, gd, weights, m, v, so_far):
    layer, start, size = chunk
    step = size // DP
    w_spec = pl.BlockSpec((1, ROWS, size), lambda o, me: (layer, me[0], (o * OWN + start) // size))
    wd_spec = pl.BlockSpec((1, step, D), lambda o, me: (layer, (me[0] * OWN + start) // step + o, 0))
    mv_spec = pl.BlockSpec((1, ROWS, size), lambda o, me: (layer, 0, (o * OWN + start) // size))
    mvd_spec = pl.BlockSpec((1, step, D), lambda o, me: (layer, start // step + o, 0))
    gu_spec = pl.BlockSpec((2, ROWS, size), lambda o, me: (0, 0, o))
    d_spec = pl.BlockSpec((step, D), lambda o, me: (o, 0))
    part, parts = (1 - layer) * PARTS + start // SIZE, size // SIZE
    ggu_spec = pl.BlockSpec((parts, 2, ROWS, SIZE), lambda o, me: (part // parts, 0, 0, o))
    gd_spec = pl.BlockSpec((step, D), lambda o, me: (part * SIZE // step + o, 0))
    mv_specs = [mv_spec, mv_spec, mvd_spec] * 2
    return pl.pallas_call(
        adamw_kernel,
        grid_spec=pltpu.PrefetchScalarGridSpec(
            num_scalar_prefetch=1,
            grid=(DP,),
            in_specs=[pl.BlockSpec(memory_space=pltpu.SMEM), ggu_spec, gd_spec, w_spec, w_spec, wd_spec, *mv_specs]
            + [pl.BlockSpec(memory_space=pl.ANY)] * len(so_far),
            out_specs=[gu_spec, d_spec, *mv_specs],
        ),
        out_shape=[jax.ShapeDtypeStruct((2, ROWS, DP * size), BF16), jax.ShapeDtypeStruct((size, D), BF16)]
        + [jax.ShapeDtypeStruct(t.shape, F32) for t in (*m, *v)],
        input_output_aliases={13 + n: 2 + n for n in range(len(so_far))},
        compiler_params=params(1),
        cost_estimate=cost(0.25, 17e6),
        name="adamw",
    )(me, factor, ggu, gd, *weights, *m, *v, *so_far)


def assemble_kernel(me_ref, gu0, d0, gu1, d1, *refs):
    wg, wu, wd = refs[-3:]
    for q, (gu, d) in enumerate(((gu0, d0), (gu1, d1))):

        @pl.when(pl.program_id(0) == q)
        def _(gu=gu, d=d):
            wg[0] = gu[0]
            wu[0] = gu[1]
            wd[0] = d[...]


def assemble(chunk, base, me, first, second, so_far):
    layer, start, size = chunk
    step = size // DP

    def when(q, r, o):
        return jnp.where(r == q, o, 0 if q else DP - 1)

    def gu_spec(q):
        return pl.BlockSpec((2, ROWS, size), lambda r, o, me: (0, 0, when(q, r, o)))

    def d_spec(q):
        return pl.BlockSpec((step, D), lambda r, o, me: (when(q, r, o), 0))

    def owner(r, me):
        return (r + base) ^ me[0]

    w_spec = pl.BlockSpec((1, ROWS, size), lambda r, o, me: (layer, owner(r, me), (o * OWN + start) // size))
    wd_spec = pl.BlockSpec((1, step, D), lambda r, o, me: (layer, (owner(r, me) * OWN + start) // step + o, 0))
    wide, tall = jax.ShapeDtypeStruct((LAYERS, D, FF), BF16), jax.ShapeDtypeStruct((LAYERS, FF, D), BF16)
    return pl.pallas_call(
        assemble_kernel,
        grid_spec=pltpu.PrefetchScalarGridSpec(
            num_scalar_prefetch=1,
            grid=(2, DP),
            in_specs=[gu_spec(0), d_spec(0), gu_spec(1), d_spec(1)] + [pl.BlockSpec(memory_space=pl.ANY)] * len(so_far),
            out_specs=[w_spec, w_spec, wd_spec],
        ),
        out_shape=[wide, wide, tall],
        input_output_aliases={5 + n: n for n in range(len(so_far))},
        compiler_params=params(2),
        cost_estimate=cost(0.15, 6e6),
        name="assemble",
    )(me, *first, *second, *so_far)


def to_core(t):
    return lax.ppermute(t, "dp", [(0, 1), (1, 0), (2, 3), (3, 2)])


def to_x(t):
    return lax.ppermute(t, "dp", [(0, 2), (2, 0), (1, 3), (3, 1)])


def solution(mesh):
    def body(x, dy, *arrays):
        weights, m, v = (arrays[i : i + 3] for i in (0, 3, 6))
        x, dy = x[0], dy[0]
        me = lax.axis_index("dp").astype(jnp.int32)[None]

        h1, a0, a1, a0t, a1t, dyt = forward(x, dy, *weights)

        gu, d, squares = backward(h1, a0, a0t, a1, a1t, dy, dyt, *weights)
        d = d.reshape(-1, D)
        total = lax.psum(jnp.sum(squares), "dp")
        factor = jnp.minimum(1.0, 0.5 * lax.rsqrt(total / COUNT + 1e-30)).reshape(1, 1)

        moments, own, near, far, last, new = (), {}, {}, {}, {}, ()
        turn = [LAST - 1, *range(LAST - 1), LAST]
        for n, k in enumerate(turn):
            own_gu, own_d, *moments = adamw(CHUNKS[k], me, factor, gu, d, weights, m, v, moments)
            own[n] = own_gu, own_d
            far[n] = tuple(map(to_x, own[n]))
            near[n] = tuple(map(to_core, own[n]))
            last[n] = tuple(map(to_core, far[n]))
        for n in range(LAST + 1):
            for ahead in (0, 1, 2) if n == 0 else (n + 2,):
                if ahead <= LAST:
                    new = assemble(CHUNKS[turn[ahead]], 0, me, own[ahead], near[ahead], new)
            new = assemble(CHUNKS[turn[n]], 2, me, far[n], last[n], new)
        return (*new, *moments)

    rows = P(None, "dp", None)
    return jax.shard_map(
        body,
        mesh=mesh,
        in_specs=(P(("rep", "dp"), None, None),) * 2 + (P(None, None, None),) * 3 + (rows,) * 6,
        out_specs=(P("rep", None, None),) * 3 + (P("rep", "dp", None),) * 6,
        check_vma=False,
    )
```

profile of v0, /device:TPU:0, one launch (start us, length us, event | category | flops | bytes accessed | tf_op | source)
XLA Modules:
  0.0 776.1 jit_solution(211467330419545878)
XLA Ops:
  0.6 66.5 %forward0.1 = (bf16[2048,512]{1,0:T(8,128)(2,1)}, bf16[2048,512]{1,0:T(8,128)(2,1)}, bf16[2048,512]{1,0:T(8,128)(2,1)}, bf16[512,2048]{1,0:T(8,128)(2,1)}, bf16[...) custom-call(bf16[2048,512]{1,0:T(8,128)(2,1)} %bitcast.14, bf16[2048,512]{1,0:T(8,128)(2,1)} %bitcast.15, ...), custom_call_target="tpu_custom_call" | custom-call | flops 51539607552 | bytes 40000000 | tf_op jit(solution)/shard_map/forward0/pallas_call | solution.py:90
  67.1 328.0 %backward.1 = (bf16[16,2,128,1024]{3,2,1,0:T(8,128)(2,1)}, bf16[16,256,512]{2,1,0:T(8,128)(2,1)}, f32[1,512]{1,0:T(1,128)}) custom-call(bf16[2048,512]{1,0:T(8,128)(2,1)} %get-tuple-element.144.h1, bf16[2048,512]{1,0:T(8,128)(2,1)} %get-tuple-element.145.a0, bf16[512,2048]{1,0:T(8,128)(2,1)} %get-tuple-element.146.a0t, ...), custom_call_target="tpu_custom_call" | custom-call | flops 240518168576 | bytes 120000000 | tf_op jit(solution)/shard_map/backward/pallas_call | solution.py:316
  396.4 6.5 psum.7
  403.6 5.2 adamw.9
  409.5 7.6 adamw.10
  417.1 7.6 adamw.11
  424.8 7.6 adamw.12
  432.4 7.6 adamw.13
  440.0 7.6 adamw.14
  447.7 7.6 adamw.15
  455.3 7.7 adamw.16
  463.0 5.3 adamw.17
  471.5 6.8 collective-permute-done.1.d0
  481.6 7.8 %collective-permute-done.44.gu0 = bf16[2,128,1024]{2,1,0:T(8,128)(2,1)S(1)} collective-permute-done((bf16[2,128,1024]{2,1,0:T(8,128)(2,1)}, bf16[2,128,1024]{2,1,0:T(8,128)(2,1)S(1)}, u32[]{:S(2)}, u32[]{:S(2)}) %collective-permute-start.44) | collective-permute-done | bytes 524320 | tf_op jit(solution)/shard_map/ppermute | solution.py:446
  491.6 9.1 %collective-permute-done.39.d0 = bf16[512,512]{1,0:T(8,128)(2,1)S(1)} collective-permute-done((bf16[512,512]{1,0:T(8,128)(2,1)}, bf16[512,512]{1,0:T(8,128)(2,1)S(1)}, u32[]{:S(2)}, u32[]{:S(2)}) %collective-permute-start.39) | collective-permute-done | bytes 524320 | tf_op jit(solution)/shard_map/ppermute | solution.py:446
  500.8 1.4 collective-permute-start.21
  502.2 9.8 %collective-permute-done.33.d0 = bf16[512,512]{1,0:T(8,128)(2,1)S(1)} collective-permute-done((bf16[512,512]{1,0:T(8,128)(2,1)}, bf16[512,512]{1,0:T(8,128)(2,1)S(1)}, u32[]{:S(2)}, u32[]{:S(2)}) %collective-permute-start.33) | collective-permute-done | bytes 524320 | tf_op jit(solution)/shard_map/ppermute | solution.py:446
  512.0 1.4 collective-permute-start.15
  513.4 9.9 %collective-permute-done.27.d0 = bf16[512,512]{1,0:T(8,128)(2,1)} collective-permute-done((bf16[512,512]{1,0:T(8,128)(2,1)}, bf16[512,512]{1,0:T(8,128)(2,1)}, u32[]{:S(2)}, u32[]{:S(2)}) %collective-permute-start.27) | collective-permute-done | bytes 524320 | tf_op jit(solution)/shard_map/ppermute | solution.py:446
  524.6 9.8 %collective-permute-done.21.d0 = bf16[512,512]{1,0:T(8,128)(2,1)S(1)} collective-permute-done((bf16[512,512]{1,0:T(8,128)(2,1)}, bf16[512,512]{1,0:T(8,128)(2,1)S(1)}, u32[]{:S(2)}, u32[]{:S(2)}) %collective-permute-start.21) | collective-permute-done | bytes 524320 | tf_op jit(solution)/shard_map/ppermute | solution.py:446
  534.5 1.4 collective-permute-start.9
  535.9 9.9 %collective-permute-done.15.d0 = bf16[512,512]{1,0:T(8,128)(2,1)} collective-permute-done((bf16[512,512]{1,0:T(8,128)(2,1)}, bf16[512,512]{1,0:T(8,128)(2,1)}, u32[]{:S(2)}, u32[]{:S(2)}) %collective-permute-start.15) | collective-permute-done | bytes 524320 | tf_op jit(solution)/shard_map/ppermute | solution.py:446
  547.9 9.0 %collective-permute-done.9.d0 = bf16[512,512]{1,0:T(8,128)(2,1)S(1)} collective-permute-done((bf16[512,512]{1,0:T(8,128)(2,1)}, bf16[512,512]{1,0:T(8,128)(2,1)S(1)}, u32[]{:S(2)}, u32[]{:S(2)}) %collective-permute-start.9) | collective-permute-done | bytes 524320 | tf_op jit(solution)/shard_map/ppermute | solution.py:446
  558.3 9.9 %collective-permute-done.5.d0 = bf16[512,512]{1,0:T(8,128)(2,1)S(1)} collective-permute-done((bf16[512,512]{1,0:T(8,128)(2,1)S(1)}, bf16[512,512]{1,0:T(8,128)(2,1)S(1)}, u32[]{:S(2)}, u32[]{:S(2)}) %collective-permute-start.5) | collective-permute-done | bytes 524320 | tf_op jit(solution)/shard_map/ppermute | solution.py:446
  572.8 17.9 %collective-permute-done.38.gu0 = bf16[2,128,2048]{2,1,0:T(8,128)(2,1)} collective-permute-done((bf16[2,128,2048]{2,1,0:T(8,128)(2,1)}, bf16[2,128,2048]{2,1,0:T(8,128)(2,1)}, u32[]{:S(2)}, u32[]{:S(2)}) %collective-permute-start.38) | collective-permute-done | bytes 1048608 | tf_op jit(solution)/shard_map/ppermute | solution.py:446
  592.6 20.5 %collective-permute-done.32.gu0 = bf16[2,128,2048]{2,1,0:T(8,128)(2,1)S(1)} collective-permute-done((bf16[2,128,2048]{2,1,0:T(8,128)(2,1)}, bf16[2,128,2048]{2,1,0:T(8,128)(2,1)S(1)}, u32[]{:S(2)}, u32[]{:S(2)}) %collective-permute-start.32) | collective-permute-done | bytes 1048608 | tf_op jit(solution)/shard_map/ppermute | solution.py:446
  616.3 5.6 assemble.18
  621.8 13.8 %collective-permute-done.26.gu0 = bf16[2,128,2048]{2,1,0:T(8,128)(2,1)} collective-permute-done((bf16[2,128,2048]{2,1,0:T(8,128)(2,1)}, bf16[2,128,2048]{2,1,0:T(8,128)(2,1)}, u32[]{:S(2)}, u32[]{:S(2)}) %collective-permute-start.26) | collective-permute-done | bytes 1048608 | tf_op jit(solution)/shard_map/ppermute | solution.py:446
  636.2 6.4 assemble.19
  642.6 6.4 assemble.20
  649.1 8.3 %collective-permute-done.20.gu0 = bf16[2,128,2048]{2,1,0:T(8,128)(2,1)} collective-permute-done((bf16[2,128,2048]{2,1,0:T(8,128)(2,1)}, bf16[2,128,2048]{2,1,0:T(8,128)(2,1)}, u32[]{:S(2)}, u32[]{:S(2)}) %collective-permute-start.20) | collective-permute-done | bytes 1048608 | tf_op jit(solution)/shard_map/ppermute | solution.py:446
  658.7 5.5 assemble.21
  664.3 6.4 assemble.22
  671.4 6.4 assemble.23
  677.8 1.4 collective-permute-start.4
  679.2 6.4 assemble.24
  685.6 6.4 assemble.25
  692.5 6.4 assemble.26
  699.0 6.4 assemble.27
  706.0 6.5 assemble.28
  712.4 14.4 %collective-permute-done.4.gu0 = bf16[2,128,2048]{2,1,0:T(8,128)(2,1)} collective-permute-done((bf16[2,128,2048]{2,1,0:T(8,128)(2,1)S(1)}, bf16[2,128,2048]{2,1,0:T(8,128)(2,1)}, u32[]{:S(2)}, u32[]{:S(2)}) %collective-permute-start.4) | collective-permute-done | bytes 1048608 | tf_op jit(solution)/shard_map/ppermute | solution.py:446
  728.2 6.4 assemble.29
  735.1 6.4 assemble.30
  742.5 6.4 assemble.31
  748.9 5.6 assemble.32
  755.9 6.4 assemble.33
  763.3 6.4 assemble.34
  770.6 5.5 assemble.35
  (167 shorter events, 35.1 us)
Async XLA Ops:
  408.8 61.5 %collective-permute-start.53 = (bf16[256,512]{1,0:T(8,128)(2,1)}, bf16[256,512]{1,0:T(8,128)(2,1)}, u32[]{:S(2)}, u32[]{:S(2)}) collective-permute-start(bf16[256,512]{1,0:T(8,128)(2,1)} %get-tuple-element.218.d0), channel_id=1, source_target_pairs={{0,1},{1,0},{2,3},{3,2},{4,5},{5,4},{6,7},{7,6}} | collective-permute-start | bytes 786440 | tf_op jit(solution)/shard_map/ppermute | solution.py:442
  408.8 61.4 %collective-permute-start.45 = (bf16[256,512]{1,0:T(8,128)(2,1)}, bf16[256,512]{1,0:T(8,128)(2,1)}, u32[]{:S(2)}, u32[]{:S(2)}) collective-permute-start(bf16[256,512]{1,0:T(8,128)(2,1)} %get-tuple-element.218.d0), channel_id=1, source_target_pairs={{0,2},{2,0},{1,3},{3,1},{4,6},{6,4},{5,7},{7,5}} | collective-permute-start | bytes 786440 | tf_op jit(solution)/shard_map/ppermute | solution.py:446
  470.8 18.7 %collective-permute-start.44 = (bf16[2,128,1024]{2,1,0:T(8,128)(2,1)}, bf16[2,128,1024]{2,1,0:T(8,128)(2,1)S(1)}, u32[]{:S(2)}, u32[]{:S(2)}) collective-permute-start(bf16[2,128,1024]{2,1,0:T(8,128)(2,1)} %get-tuple-element.217.gu0), channel_id=1, source_target_pairs={{0,2},{2,0},{1,3},{3,1},{4,6},{6,4},{5,7},{7,5}} | collective-permute-start | bytes 1572872 | tf_op jit(solution)/shard_map/ppermute | solution.py:446
  479.0 11.9 %collective-permute-start.43 = (bf16[512,512]{1,0:T(8,128)(2,1)}, bf16[512,512]{1,0:T(8,128)(2,1)S(1)}, u32[]{:S(2)}, u32[]{:S(2)}) collective-permute-start(bf16[512,512]{1,0:T(8,128)(2,1)} %get-tuple-element.212.d0), channel_id=1, source_target_pairs={{0,1},{1,0},{2,3},{3,2},{4,5},{5,4},{6,7},{7,6}} | collective-permute-start | bytes 1572872 | tf_op jit(solution)/shard_map/ppermute | solution.py:442
  479.0 11.9 %collective-permute-start.47 = (bf16[256,512]{1,0:T(8,128)(2,1)}, bf16[256,512]{1,0:T(8,128)(2,1)S(1)}, u32[]{:S(2)}, u32[]{:S(2)}) collective-permute-start(bf16[256,512]{1,0:T(8,128)(2,1)} %collective-permute-done.45.d0), channel_id=1, source_target_pairs={{0,1},{1,0},{2,3},{3,2},{4,5},{5,4},{6,7},{7,6}} | collective-permute-start | bytes 786440 | tf_op jit(solution)/shard_map/ppermute | solution.py:442
  479.5 21.2 %collective-permute-start.39 = (bf16[512,512]{1,0:T(8,128)(2,1)}, bf16[512,512]{1,0:T(8,128)(2,1)S(1)}, u32[]{:S(2)}, u32[]{:S(2)}) collective-permute-start(bf16[512,512]{1,0:T(8,128)(2,1)} %get-tuple-element.216.d0), channel_id=1, source_target_pairs={{0,2},{2,0},{1,3},{3,1},{4,6},{6,4},{5,7},{7,5}} | collective-permute-start | bytes 1572872 | tf_op jit(solution)/shard_map/ppermute | solution.py:446
  481.6 19.1 %collective-permute-start.37 = (bf16[512,512]{1,0:T(8,128)(2,1)}, bf16[512,512]{1,0:T(8,128)(2,1)S(1)}, u32[]{:S(2)}, u32[]{:S(2)}) collective-permute-start(bf16[512,512]{1,0:T(8,128)(2,1)} %get-tuple-element.210.d0), channel_id=1, source_target_pairs={{0,1},{1,0},{2,3},{3,2},{4,5},{5,4},{6,7},{7,6}} | collective-permute-start | bytes 1572872 | tf_op jit(solution)/shard_map/ppermute | solution.py:442
  489.5 22.5 %collective-permute-start.33 = (bf16[512,512]{1,0:T(8,128)(2,1)}, bf16[512,512]{1,0:T(8,128)(2,1)S(1)}, u32[]{:S(2)}, u32[]{:S(2)}) collective-permute-start(bf16[512,512]{1,0:T(8,128)(2,1)} %get-tuple-element.214.d0), channel_id=1, source_target_pairs={{0,2},{2,0},{1,3},{3,1},{4,6},{6,4},{5,7},{7,5}} | collective-permute-start | bytes 1572872 | tf_op jit(solution)/shard_map/ppermute | solution.py:446
  490.9 21.1 %collective-permute-start.31 = (bf16[512,512]{1,0:T(8,128)(2,1)}, bf16[512,512]{1,0:T(8,128)(2,1)S(1)}, u32[]{:S(2)}, u32[]{:S(2)}) collective-permute-start(bf16[512,512]{1,0:T(8,128)(2,1)} %get-tuple-element.208.d0), channel_id=1, source_target_pairs={{0,1},{1,0},{2,3},{3,2},{4,5},{5,4},{6,7},{7,6}} | collective-permute-start | bytes 1572872 | tf_op jit(solution)/shard_map/ppermute | solution.py:442
  490.9 32.4 %collective-permute-start.27 = (bf16[512,512]{1,0:T(8,128)(2,1)}, bf16[512,512]{1,0:T(8,128)(2,1)}, u32[]{:S(2)}, u32[]{:S(2)}) collective-permute-start(bf16[512,512]{1,0:T(8,128)(2,1)} %get-tuple-element.212.d0), channel_id=1, source_target_pairs={{0,2},{2,0},{1,3},{3,1},{4,6},{6,4},{5,7},{7,5}} | collective-permute-start | bytes 1572872 | tf_op jit(solution)/shard_map/ppermute | solution.py:446
  500.7 22.6 %collective-permute-start.25 = (bf16[512,512]{1,0:T(8,128)(2,1)}, bf16[512,512]{1,0:T(8,128)(2,1)S(1)}, u32[]{:S(2)}, u32[]{:S(2)}) collective-permute-start(bf16[512,512]{1,0:T(8,128)(2,1)} %get-tuple-element.206.d0), channel_id=1, source_target_pairs={{0,1},{1,0},{2,3},{3,2},{4,5},{5,4},{6,7},{7,6}} | collective-permute-start | bytes 1572872 | tf_op jit(solution)/shard_map/ppermute | solution.py:442
  500.8 33.7 %collective-permute-start.21 = (bf16[512,512]{1,0:T(8,128)(2,1)}, bf16[512,512]{1,0:T(8,128)(2,1)S(1)}, u32[]{:S(2)}, u32[]{:S(2)}) collective-permute-start(bf16[512,512]{1,0:T(8,128)(2,1)} %get-tuple-element.210.d0), channel_id=1, source_target_pairs={{0,2},{2,0},{1,3},{3,1},{4,6},{6,4},{5,7},{7,5}} | collective-permute-start | bytes 1572872 | tf_op jit(solution)/shard_map/ppermute | solution.py:446
  512.0 22.5 %collective-permute-start.19 = (bf16[512,512]{1,0:T(8,128)(2,1)S(1)}, bf16[512,512]{1,0:T(8,128)(2,1)S(1)}, u32[]{:S(2)}, u32[]{:S(2)}) collective-permute-start(bf16[512,512]{1,0:T(8,128)(2,1)S(1)} %copy-done.13), channel_id=1, source_target_pairs={{0,1},{1,0},{2,3},{3,2},{4,5},{5,4},{6,7},{7,6}} | collective-permute-start | bytes 1572872 | tf_op jit(solution)/shard_map/ppermute | solution.py:442
  512.0 33.8 %collective-permute-start.15 = (bf16[512,512]{1,0:T(8,128)(2,1)}, bf16[512,512]{1,0:T(8,128)(2,1)}, u32[]{:S(2)}, u32[]{:S(2)}) collective-permute-start(bf16[512,512]{1,0:T(8,128)(2,1)} %get-tuple-element.208.d0), channel_id=1, source_target_pairs={{0,2},{2,0},{1,3},{3,1},{4,6},{6,4},{5,7},{7,5}} | collective-permute-start | bytes 1572872 | tf_op jit(solution)/shard_map/ppermute | solution.py:446
  523.3 44.8 %collective-permute-start.50 = (bf16[2,128,2048]{2,1,0:T(8,128)(2,1)}, bf16[2,128,2048]{2,1,0:T(8,128)(2,1)S(1)}, u32[]{:S(2)}, u32[]{:S(2)}) collective-permute-start(bf16[2,128,2048]{2,1,0:T(8,128)(2,1)} %get-tuple-element.215.gu0), channel_id=1, source_target_pairs={{0,1},{1,0},{2,3},{3,2},{4,5},{5,4},{6,7},{7,6}} | collective-permute-start | bytes 3145736 | tf_op jit(solution)/shard_map/ppermute | solution.py:442
  524.1 23.0 %collective-permute-start.12 = (bf16[2,128,1024]{2,1,0:T(8,128)(2,1)}, bf16[2,128,1024]{2,1,0:T(8,128)(2,1)S(1)}, u32[]{:S(2)}, u32[]{:S(2)}) collective-permute-start(bf16[2,128,1024]{2,1,0:T(8,128)(2,1)} %get-tuple-element.201.gu0), channel_id=1, source_target_pairs={{0,1},{1,0},{2,3},{3,2},{4,5},{5,4},{6,7},{7,6}} | collective-permute-start | bytes 1572872 | tf_op jit(solution)/shard_map/ppermute | solution.py:442
  534.4 35.5 %collective-permute-start.48 = (bf16[2,128,2048]{2,1,0:T(8,128)(2,1)}, bf16[2,128,2048]{2,1,0:T(8,128)(2,1)S(1)}, u32[]{:S(2)}, u32[]{:S(2)}) collective-permute-start(bf16[2,128,2048]{2,1,0:T(8,128)(2,1)} %get-tuple-element.213.gu0), channel_id=1, source_target_pairs={{0,1},{1,0},{2,3},{3,2},{4,5},{5,4},{6,7},{7,6}} | collective-permute-start | bytes 3145736 | tf_op jit(solution)/shard_map/ppermute | solution.py:442
  534.5 22.4 %collective-permute-start.9 = (bf16[512,512]{1,0:T(8,128)(2,1)}, bf16[512,512]{1,0:T(8,128)(2,1)S(1)}, u32[]{:S(2)}, u32[]{:S(2)}) collective-permute-start(bf16[512,512]{1,0:T(8,128)(2,1)} %get-tuple-element.206.d0), channel_id=1, source_target_pairs={{0,2},{2,0},{1,3},{3,1},{4,6},{6,4},{5,7},{7,5}} | collective-permute-start | bytes 1572872 | tf_op jit(solution)/shard_map/ppermute | solution.py:446
  545.8 22.4 %collective-permute-start.5 = (bf16[512,512]{1,0:T(8,128)(2,1)S(1)}, bf16[512,512]{1,0:T(8,128)(2,1)S(1)}, u32[]{:S(2)}, u32[]{:S(2)}) collective-permute-start(bf16[512,512]{1,0:T(8,128)(2,1)S(1)} %copy-done.13), channel_id=1, source_target_pairs={{0,2},{2,0},{1,3},{3,1},{4,6},{6,4},{5,7},{7,5}} | collective-permute-start | bytes 1572872 | tf_op jit(solution)/shard_map/ppermute | solution.py:446
  547.9 23.4 %collective-permute-start.42 = (bf16[2,128,2048]{2,1,0:T(8,128)(2,1)}, bf16[2,128,2048]{2,1,0:T(8,128)(2,1)S(1)}, u32[]{:S(2)}, u32[]{:S(2)}) collective-permute-start(bf16[2,128,2048]{2,1,0:T(8,128)(2,1)} %get-tuple-element.211.gu0), channel_id=1, source_target_pairs={{0,1},{1,0},{2,3},{3,2},{4,5},{5,4},{6,7},{7,6}} | collective-permute-start | bytes 3145736 | tf_op jit(solution)/shard_map/ppermute | solution.py:442
  556.9 33.8 %collective-permute-start.38 = (bf16[2,128,2048]{2,1,0:T(8,128)(2,1)}, bf16[2,128,2048]{2,1,0:T(8,128)(2,1)}, u32[]{:S(2)}, u32[]{:S(2)}) collective-permute-start(bf16[2,128,2048]{2,1,0:T(8,128)(2,1)} %get-tuple-element.215.gu0), channel_id=1, source_target_pairs={{0,2},{2,0},{1,3},{3,1},{4,6},{6,4},{5,7},{7,5}} | collective-permute-start | bytes 3145736 | tf_op jit(solution)/shard_map/ppermute | solution.py:446
  569.0 23.1 %collective-permute-start.36 = (bf16[2,128,2048]{2,1,0:T(8,128)(2,1)}, bf16[2,128,2048]{2,1,0:T(8,128)(2,1)S(1)}, u32[]{:S(2)}, u32[]{:S(2)}) collective-permute-start(bf16[2,128,2048]{2,1,0:T(8,128)(2,1)} %get-tuple-element.209.gu0), channel_id=1, source_target_pairs={{0,1},{1,0},{2,3},{3,2},{4,5},{5,4},{6,7},{7,6}} | collective-permute-start | bytes 3145736 | tf_op jit(solution)/shard_map/ppermute | solution.py:442
  569.9 43.1 %collective-permute-start.32 = (bf16[2,128,2048]{2,1,0:T(8,128)(2,1)}, bf16[2,128,2048]{2,1,0:T(8,128)(2,1)S(1)}, u32[]{:S(2)}, u32[]{:S(2)}) collective-permute-start(bf16[2,128,2048]{2,1,0:T(8,128)(2,1)} %get-tuple-element.213.gu0), channel_id=1, source_target_pairs={{0,2},{2,0},{1,3},{3,1},{4,6},{6,4},{5,7},{7,5}} | collective-permute-start | bytes 3145736 | tf_op jit(solution)/shard_map/ppermute | solution.py:446
  571.3 20.8 %collective-permute-start.41 = (bf16[512,512]{1,0:T(8,128)(2,1)S(1)}, bf16[512,512]{1,0:T(8,128)(2,1)}, u32[]{:S(2)}, u32[]{:S(2)}) collective-permute-start(bf16[512,512]{1,0:T(8,128)(2,1)S(1)} %collective-permute-done.39.d0), channel_id=1, source_target_pairs={{0,1},{1,0},{2,3},{3,2},{4,5},{5,4},{6,7},{7,6}} | collective-permute-start | bytes 1572872 | tf_op jit(solution)/shard_map/ppermute | solution.py:442
  572.5 42.0 %collective-permute-start.30 = (bf16[2,128,2048]{2,1,0:T(8,128)(2,1)S(1)}, bf16[2,128,2048]{2,1,0:T(8,128)(2,1)S(1)}, u32[]{:S(2)}, u32[]{:S(2)}) collective-permute-start(bf16[2,128,2048]{2,1,0:T(8,128)(2,1)S(1)} %copy-done.2), channel_id=1, source_target_pairs={{0,1},{1,0},{2,3},{3,2},{4,5},{5,4},{6,7},{7,6}} | collective-permute-start | bytes 3145736 | tf_op jit(solution)/shard_map/ppermute | solution.py:442
  590.7 44.9 %collective-permute-start.26 = (bf16[2,128,2048]{2,1,0:T(8,128)(2,1)}, bf16[2,128,2048]{2,1,0:T(8,128)(2,1)}, u32[]{:S(2)}, u32[]{:S(2)}) collective-permute-start(bf16[2,128,2048]{2,1,0:T(8,128)(2,1)} %get-tuple-element.211.gu0), channel_id=1, source_target_pairs={{0,2},{2,0},{1,3},{3,1},{4,6},{6,4},{5,7},{7,5}} | collective-permute-start | bytes 3145736 | tf_op jit(solution)/shard_map/ppermute | solution.py:446
  592.1 22.4 %collective-permute-start.35 = (bf16[512,512]{1,0:T(8,128)(2,1)S(1)}, bf16[512,512]{1,0:T(8,128)(2,1)S(1)}, u32[]{:S(2)}, u32[]{:S(2)}) collective-permute-start(bf16[512,512]{1,0:T(8,128)(2,1)S(1)} %collective-permute-done.33.d0), channel_id=1, source_target_pairs={{0,1},{1,0},{2,3},{3,2},{4,5},{5,4},{6,7},{7,6}} | collective-permute-start | bytes 1572872 | tf_op jit(solution)/shard_map/ppermute | solution.py:442
  592.1 44.1 %collective-permute-start.24 = (bf16[2,128,2048]{2,1,0:T(8,128)(2,1)S(1)}, bf16[2,128,2048]{2,1,0:T(8,128)(2,1)}, u32[]{:S(2)}, u32[]{:S(2)}) collective-permute-start(bf16[2,128,2048]{2,1,0:T(8,128)(2,1)S(1)} %copy-done.1), channel_id=1, source_target_pairs={{0,1},{1,0},{2,3},{3,2},{4,5},{5,4},{6,7},{7,6}} | collective-permute-start | bytes 3145736 | tf_op jit(solution)/shard_map/ppermute | solution.py:442
  613.1 44.3 %collective-permute-start.20 = (bf16[2,128,2048]{2,1,0:T(8,128)(2,1)}, bf16[2,128,2048]{2,1,0:T(8,128)(2,1)}, u32[]{:S(2)}, u32[]{:S(2)}) collective-permute-start(bf16[2,128,2048]{2,1,0:T(8,128)(2,1)} %get-tuple-element.209.gu0), channel_id=1, source_target_pairs={{0,2},{2,0},{1,3},{3,1},{4,6},{6,4},{5,7},{7,5}} | collective-permute-start | bytes 3145736 | tf_op jit(solution)/shard_map/ppermute | solution.py:446
  614.5 21.2 %collective-permute-start.29 = (bf16[512,512]{1,0:T(8,128)(2,1)}, bf16[512,512]{1,0:T(8,128)(2,1)}, u32[]{:S(2)}, u32[]{:S(2)}) collective-permute-start(bf16[512,512]{1,0:T(8,128)(2,1)} %collective-permute-done.27.d0), channel_id=1, source_target_pairs={{0,1},{1,0},{2,3},{3,2},{4,5},{5,4},{6,7},{7,6}} | collective-permute-start | bytes 1572872 | tf_op jit(solution)/shard_map/ppermute | solution.py:442
  616.3 54.5 %collective-permute-start.40 = (bf16[2,128,2048]{2,1,0:T(8,128)(2,1)}, bf16[2,128,2048]{2,1,0:T(8,128)(2,1)}, u32[]{:S(2)}, u32[]{:S(2)}) collective-permute-start(bf16[2,128,2048]{2,1,0:T(8,128)(2,1)} %collective-permute-done.38.gu0), channel_id=1, source_target_pairs={{0,1},{1,0},{2,3},{3,2},{4,5},{5,4},{6,7},{7,6}} | collective-permute-start | bytes 3145736 | tf_op jit(solution)/shard_map/ppermute | solution.py:442
  635.7 42.1 %collective-permute-start.18 = (bf16[2,128,2048]{2,1,0:T(8,128)(2,1)S(1)}, bf16[2,128,2048]{2,1,0:T(8,128)(2,1)}, u32[]{:S(2)}, u32[]{:S(2)}) collective-permute-start(bf16[2,128,2048]{2,1,0:T(8,128)(2,1)S(1)} %copy-done), channel_id=1, source_target_pairs={{0,1},{1,0},{2,3},{3,2},{4,5},{5,4},{6,7},{7,6}} | collective-permute-start | bytes 3145736 | tf_op jit(solution)/shard_map/ppermute | solution.py:442
  635.7 28.6 %collective-permute-start.23 = (bf16[512,512]{1,0:T(8,128)(2,1)S(1)}, bf16[512,512]{1,0:T(8,128)(2,1)}, u32[]{:S(2)}, u32[]{:S(2)}) collective-permute-start(bf16[512,512]{1,0:T(8,128)(2,1)S(1)} %copy-done.19), channel_id=1, source_target_pairs={{0,1},{1,0},{2,3},{3,2},{4,5},{5,4},{6,7},{7,6}} | collective-permute-start | bytes 1572872 | tf_op jit(solution)/shard_map/ppermute | solution.py:442
  636.2 43.0 %collective-permute-start.34 = (bf16[2,128,2048]{2,1,0:T(8,128)(2,1)}, bf16[2,128,2048]{2,1,0:T(8,128)(2,1)}, u32[]{:S(2)}, u32[]{:S(2)}) collective-permute-start(bf16[2,128,2048]{2,1,0:T(8,128)(2,1)} %copy-done.4), channel_id=1, source_target_pairs={{0,1},{1,0},{2,3},{3,2},{4,5},{5,4},{6,7},{7,6}} | collective-permute-start | bytes 3145736 | tf_op jit(solution)/shard_map/ppermute | solution.py:442
  657.4 34.7 %collective-permute-start.14 = (bf16[2,128,2048]{2,1,0:T(8,128)(2,1)S(1)}, bf16[2,128,2048]{2,1,0:T(8,128)(2,1)}, u32[]{:S(2)}, u32[]{:S(2)}) collective-permute-start(bf16[2,128,2048]{2,1,0:T(8,128)(2,1)S(1)} %copy-done.2), channel_id=1, source_target_pairs={{0,2},{2,0},{1,3},{3,1},{4,6},{6,4},{5,7},{7,5}} | collective-permute-start | bytes 3145736 | tf_op jit(solution)/shard_map/ppermute | solution.py:446
  664.3 34.6 %collective-permute-start.28 = (bf16[2,128,2048]{2,1,0:T(8,128)(2,1)}, bf16[2,128,2048]{2,1,0:T(8,128)(2,1)}, u32[]{:S(2)}, u32[]{:S(2)}) collective-permute-start(bf16[2,128,2048]{2,1,0:T(8,128)(2,1)} %collective-permute-done.26.gu0), channel_id=1, source_target_pairs={{0,1},{1,0},{2,3},{3,2},{4,5},{5,4},{6,7},{7,6}} | collective-permute-start | bytes 3145736 | tf_op jit(solution)/shard_map/ppermute | solution.py:442
  670.7 35.2 %collective-permute-start.8 = (bf16[2,128,2048]{2,1,0:T(8,128)(2,1)S(1)}, bf16[2,128,2048]{2,1,0:T(8,128)(2,1)}, u32[]{:S(2)}, u32[]{:S(2)}) collective-permute-start(bf16[2,128,2048]{2,1,0:T(8,128)(2,1)S(1)} %copy-done.1), channel_id=1, source_target_pairs={{0,2},{2,0},{1,3},{3,1},{4,6},{6,4},{5,7},{7,5}} | collective-permute-start | bytes 3145736 | tf_op jit(solution)/shard_map/ppermute | solution.py:446
  677.8 49.0 %collective-permute-start.4 = (bf16[2,128,2048]{2,1,0:T(8,128)(2,1)S(1)}, bf16[2,128,2048]{2,1,0:T(8,128)(2,1)}, u32[]{:S(2)}, u32[]{:S(2)}) collective-permute-start(bf16[2,128,2048]{2,1,0:T(8,128)(2,1)S(1)} %copy-done), channel_id=1, source_target_pairs={{0,2},{2,0},{1,3},{3,1},{4,6},{6,4},{5,7},{7,5}} | collective-permute-start | bytes 3145736 | tf_op jit(solution)/shard_map/ppermute | solution.py:446
  679.2 49.0 %collective-permute-start.22 = (bf16[2,128,2048]{2,1,0:T(8,128)(2,1)}, bf16[2,128,2048]{2,1,0:T(8,128)(2,1)}, u32[]{:S(2)}, u32[]{:S(2)}) collective-permute-start(bf16[2,128,2048]{2,1,0:T(8,128)(2,1)} %collective-permute-done.20.gu0), channel_id=1, source_target_pairs={{0,1},{1,0},{2,3},{3,2},{4,5},{5,4},{6,7},{7,6}} | collective-permute-start | bytes 3145736 | tf_op jit(solution)/shard_map/ppermute | solution.py:442
  692.1 49.4 %collective-permute-start.16 = (bf16[2,128,2048]{2,1,0:T(8,128)(2,1)}, bf16[2,128,2048]{2,1,0:T(8,128)(2,1)S(1)}, u32[]{:S(2)}, u32[]{:S(2)}) collective-permute-start(bf16[2,128,2048]{2,1,0:T(8,128)(2,1)} %collective-permute-done.14.gu0), channel_id=1, source_target_pairs={{0,1},{1,0},{2,3},{3,2},{4,5},{5,4},{6,7},{7,6}} | collective-permute-start | bytes 3145736 | tf_op jit(solution)/shard_map/ppermute | solution.py:442
  698.9 35.7 %collective-permute-start.17 = (bf16[512,512]{1,0:T(8,128)(2,1)}, bf16[512,512]{1,0:T(8,128)(2,1)}, u32[]{:S(2)}, u32[]{:S(2)}) collective-permute-start(bf16[512,512]{1,0:T(8,128)(2,1)} %collective-permute-done.15.d0), channel_id=1, source_target_pairs={{0,1},{1,0},{2,3},{3,2},{4,5},{5,4},{6,7},{7,6}} | collective-permute-start | bytes 1572872 | tf_op jit(solution)/shard_map/ppermute | solution.py:442
  706.0 49.0 %collective-permute-start.10 = (bf16[2,128,2048]{2,1,0:T(8,128)(2,1)}, bf16[2,128,2048]{2,1,0:T(8,128)(2,1)S(1)}, u32[]{:S(2)}, u32[]{:S(2)}) collective-permute-start(bf16[2,128,2048]{2,1,0:T(8,128)(2,1)} %collective-permute-done.8.gu0), channel_id=1, source_target_pairs={{0,1},{1,0},{2,3},{3,2},{4,5},{5,4},{6,7},{7,6}} | collective-permute-start | bytes 3145736 | tf_op jit(solution)/shard_map/ppermute | solution.py:442
  726.8 22.0 %collective-permute-start = (bf16[2,128,1024]{2,1,0:T(8,128)(2,1)S(1)}, bf16[2,128,1024]{2,1,0:T(8,128)(2,1)}, u32[]{:S(2)}, u32[]{:S(2)}) collective-permute-start(bf16[2,128,1024]{2,1,0:T(8,128)(2,1)S(1)} %copy-done.12), channel_id=1, source_target_pairs={{0,2},{2,0},{1,3},{3,1},{4,6},{6,4},{5,7},{7,5}} | collective-permute-start | bytes 1572872 | tf_op jit(solution)/shard_map/ppermute | solution.py:446
  728.2 34.1 %collective-permute-start.6 = (bf16[2,128,2048]{2,1,0:T(8,128)(2,1)}, bf16[2,128,2048]{2,1,0:T(8,128)(2,1)S(1)}, u32[]{:S(2)}, u32[]{:S(2)}) collective-permute-start(bf16[2,128,2048]{2,1,0:T(8,128)(2,1)} %collective-permute-done.4.gu0), channel_id=1, source_target_pairs={{0,1},{1,0},{2,3},{3,2},{4,5},{5,4},{6,7},{7,6}} | collective-permute-start | bytes 3145736 | tf_op jit(solution)/shard_map/ppermute | solution.py:442
  734.6 19.9 %collective-permute-start.11 = (bf16[512,512]{1,0:T(8,128)(2,1)}, bf16[512,512]{1,0:T(8,128)(2,1)}, u32[]{:S(2)}, u32[]{:S(2)}) collective-permute-start(bf16[512,512]{1,0:T(8,128)(2,1)} %copy-done.15), channel_id=1, source_target_pairs={{0,1},{1,0},{2,3},{3,2},{4,5},{5,4},{6,7},{7,6}} | collective-permute-start | bytes 1572872 | tf_op jit(solution)/shard_map/ppermute | solution.py:442
  741.5 20.8 %collective-permute-start.7 = (bf16[512,512]{1,0:T(8,128)(2,1)}, bf16[512,512]{1,0:T(8,128)(2,1)}, u32[]{:S(2)}, u32[]{:S(2)}) collective-permute-start(bf16[512,512]{1,0:T(8,128)(2,1)} %copy-done.14), channel_id=1, source_target_pairs={{0,1},{1,0},{2,3},{3,2},{4,5},{5,4},{6,7},{7,6}} | collective-permute-start | bytes 1572872 | tf_op jit(solution)/shard_map/ppermute | solution.py:442
  748.8 20.9 %collective-permute-start.2 = (bf16[2,128,1024]{2,1,0:T(8,128)(2,1)}, bf16[2,128,1024]{2,1,0:T(8,128)(2,1)S(1)}, u32[]{:S(2)}, u32[]{:S(2)}) collective-permute-start(bf16[2,128,1024]{2,1,0:T(8,128)(2,1)} %collective-permute-done.gu0), channel_id=1, source_target_pairs={{0,1},{1,0},{2,3},{3,2},{4,5},{5,4},{6,7},{7,6}} | collective-permute-start | bytes 1572872 | tf_op jit(solution)/shard_map/ppermute | solution.py:442
  754.5 15.1 %collective-permute-start.3 = (bf16[256,512]{1,0:T(8,128)(2,1)S(1)}, bf16[256,512]{1,0:T(8,128)(2,1)S(1)}, u32[]{:S(2)}, u32[]{:S(2)}) collective-permute-start(bf16[256,512]{1,0:T(8,128)(2,1)S(1)} %copy-done.33), channel_id=1, source_target_pairs={{0,1},{1,0},{2,3},{3,2},{4,5},{5,4},{6,7},{7,6}} | collective-permute-start | bytes 786440 | tf_op jit(solution)/shard_map/ppermute | solution.py:442
  (44 other events, 1309.7 us)
where the time goes:
time: 779 us; the launch traced here: 776 us
  Pallas kernels  570 us (73%)
  waiting for transfers between devices  158 us (20%)
  starting transfers between devices  27.2 us (3%)
  local copies, waits for them, and re-layouts  11.5 us (1%)
    pallas_call x1, Pallas kernels, backward(): pl.pallas_call(backward_kernel, grid=(STEPS,), in_specs=[pl.BlockSpec(mem...  328 us
    ppermute x18, waiting for transfers between devices, to_x(): return lax.ppermute(t, 'dp', [(0, 2), (2, 0), (1, 3), (3, 1)])  157 us
    pallas_call x18, Pallas kernels, assemble(): pl.pallas_call(assemble_kernel, grid_spec=pltpu.PrefetchScalarGridSpec(nu...  112 us
    pallas_call x1, Pallas kernels, forward(): pl.pallas_call(forward_kernel, grid=(FF // FT, TOKENS // FI), in_specs=[w...  66.5 us
    pallas_call x9, Pallas kernels, adamw(): pl.pallas_call(adamw_kernel, grid_spec=pltpu.PrefetchScalarGridSpec(num_s...  63.9 us
    ppermute x18, starting transfers between devices, to_x(): return lax.ppermute(t, 'dp', [(0, 2), (2, 0), (1, 3), (3, 1)])  22 us
  transfers between devices with their start and end apart: 54, of which 15 were waited for; matrix products, arithmetic and copies ran while one was open for 0% of the time, Pallas kernels for 21%

commit v1 on v0

--- a/solution.py
+++ b/solution.py
@@ -1,3 +1,5 @@
+import functools
+
 import jax
 import jax.numpy as jnp
 from jax import lax
@@ -112,11 +114,12 @@
 def backward_kernel(
     h1, a0, a0t, a1, a1t, dy0, dy0t, wg, wu, wd, gu_out, d_out, squares,
     a, at, dy, dyt, h, da, wgu_buf, wd_buf, z, dgu, dt, grads,
-    own_gu, far_gu, give_gu, core_gu, x_gu, own_d, far_d, give_d, core_d, x_d,
-    w_sem, in_sem, core_send, core_recv, x_send, x_recv, out_sem, core_free, x_free,
+    own_gu, far_gu, give_gu, core_gu, x_gu, own_d, far_d, give_d, core_d, x_d, sq,
+    w_sem, in_sem, core_send, core_recv, x_send, x_recv, out_sem, sq_send, sq_recv, core_free, x_free,
 ):
     t = pl.program_id(0)
-    part, r = lax.div(t, DP), lax.rem(t, DP)
+    part, turn = lax.div(t, DP), lax.rem(t, DP)
+    r = lax.rem(turn + 2, DP)
     slot = lax.rem(part, SLOTS)
     rep, me = lax.axis_index("rep"), lax.axis_index("dp")
     mx, mc = lax.div(me, 2), lax.rem(me, 2)
@@ -128,7 +131,7 @@
     mesh_id = pl.DeviceIdType.MESH
 
     def weights(t):
-        part, r = lax.div(t, DP), lax.rem(t, DP)
+        part, r = lax.div(t, DP), lax.rem(t + 2, DP)
         layer = 1 - lax.div(part, PARTS)
         at_ff = pl.multiple_of(related(lax.div(r, 2), lax.rem(r, 2)) * OWN + lax.rem(part, PARTS) * SIZE, SIZE)
         n = lax.rem(t, 2)
@@ -142,53 +145,61 @@
         pairs = zip(sources, (a, at, dy, dyt, h))
         return [pltpu.make_async_copy(src, dst, in_sem.at[n]) for n, (src, dst) in enumerate(pairs)]
 
-    def to_core(n):
-        return [
-            pltpu.make_async_remote_copy(src.at[n], dst.at[n], core_send.at[n, i], core_recv.at[n, i], device_id=core_peer, device_id_type=mesh_id)
-            for i, (src, dst) in enumerate(((give_gu, core_gu), (give_d, core_d)))
-        ]
-
-    def to_x(n):
-        return [
-            pltpu.make_async_remote_copy(src.at[n], dst.at[n], x_send.at[n, i], x_recv.at[n, i], device_id=x_peer, device_id_type=mesh_id)
-            for i, (src, dst) in enumerate(((far_gu, x_gu), (far_d, x_d)))
-        ]
+    def columns_of(half):
+        return pl.ds(pl.multiple_of((mx if half else 1 - mx) * 2 * SIZE, 2 * SIZE), 2 * SIZE)
+
+    def remote(src, dst, send, recv, peer):
+        return pltpu.make_async_remote_copy(src, dst, send, recv, device_id=peer, device_id_type=mesh_id)
+
+    def to_core(n, half):
+        c = columns_of(half)
+        pairs = ((give_gu.at[n, :, :, :, c], core_gu.at[n, :, :, :, c]), (give_d.at[n, 1 - half], core_d.at[n, 1 - half]))
+        return [remote(src, dst, core_send.at[n, half, i], core_recv.at[n, half, i], core_peer) for i, (src, dst) in enumerate(pairs)]
+
+    def to_x(n, half):
+        c = columns_of(half)
+        pairs = ((far_gu.at[n, :, :, c], x_gu.at[n, :, :, c]), (far_d.at[n], x_d.at[n]))[: 2 - half]
+        return [remote(src, dst, x_send.at[n, half, i], x_recv.at[n, half, i], x_peer) for i, (src, dst) in enumerate(pairs)]
 
     def out(p, n):
         return [
             pltpu.make_async_copy(src.at[n], dst.at[p], out_sem.at[n, i]) for i, (src, dst) in enumerate(((own_gu, gu_out), (own_d, d_out)))
         ]
 
-    def give(p):
+    def give(p, half):
         n = lax.rem(p, SLOTS)
-
-        @pl.when(p >= SLOTS)
-        def _():
-            pl.semaphore_wait(core_free, 1)
-
-        for copy in to_core(n):
-            copy.start()
-
-    def pair(p):
+        if half == 0:
+
+            @pl.when(p >= SLOTS)
+            def _():
+                pl.semaphore_wait(core_free, 1)
+
+        for copy in to_core(n, half):
+            copy.start()
+
+    def pair(p, half):
         n = lax.rem(p, SLOTS)
-        for copy in to_core(n):
+        for copy in to_core(n, half):
             copy.wait_recv()
-        far_gu[n] = (far_gu[n].astype(F32) + core_gu[n, 1].astype(F32)).astype(BF16)
-        far_d[n] = (far_d[n].astype(F32) + core_d[n, 1].astype(F32)).astype(BF16)
-
-        @pl.when(p >= SLOTS)
-        def _():
-            pl.semaphore_wait(x_free, 1)
-
-        for copy in to_x(n):
+        c = columns_of(half)
+        far_gu[n, :, :, c] = (far_gu[n, :, :, c].astype(F32) + core_gu[n, 1, :, :, c].astype(F32)).astype(BF16)
+        if half == 0:
+            far_d[n] = (far_d[n].astype(F32) + core_d[n, 1].astype(F32)).astype(BF16)
+
+            @pl.when(p >= SLOTS)
+            def _():
+                pl.semaphore_wait(x_free, 1)
+
+        for copy in to_x(n, half):
             copy.start()
 
     def finish(p):
         n = lax.rem(p, SLOTS)
-        for copy in to_x(n):
-            copy.wait()
-        for copy in to_core(n):
-            copy.wait_send()
+        for half in range(2):
+            for copy in to_x(n, half):
+                copy.wait()
+            for copy in to_core(n, half):
+                copy.wait_send()
         total = (own_gu[n].astype(F32) + core_gu[n, 0].astype(F32) + x_gu[n].astype(F32)).astype(BF16)
         own_gu[n] = total
         total = total.astype(F32)
@@ -197,7 +208,7 @@
         total = (own_d[n].astype(F32) + core_d[n, 0].astype(F32) + x_d[n].astype(F32)).astype(BF16)
         own_d[n] = total
         total = total.astype(F32)
-        squares[...] += line + jnp.sum(total * total, 0, keepdims=True)
+        sq[0, 0:1, :] += line + jnp.sum(total * total, 0, keepdims=True)
 
         @pl.when(p < LAYERS * PARTS - SLOTS)
         def _():
@@ -215,7 +226,7 @@
         for copy in (*weights(t), *inputs(a1, a1t, dy0, dy0t, h1)):
             copy.start()
         da[...] = jnp.zeros_like(da)
-        squares[...] = jnp.zeros_like(squares)
+        sq[...] = jnp.zeros_like(sq)
         for copy in inputs(a1, a1t, dy0, dy0t, h1):
             copy.wait()
         pl.semaphore_wait(barrier, 2)
@@ -281,28 +292,44 @@
         def _(d=d):
             d[slot] = dt[...]
 
-    @pl.when((r == 0) & (part >= 1))
-    def _():
-        pair(part - 1)
-
-    @pl.when((r == 2) & (part >= 2))
+    @pl.when((turn == 0) & (part >= 1))
+    def _():
+        pair(part - 1, 1)
+
+    @pl.when(turn == 1)
+    def _():
+        give(part, 0)
+
+    @pl.when((turn == 1) & (part >= 2))
     def _():
         finish(part - 2)
 
-    @pl.when((r == 3) & (part >= 2))
+    @pl.when(turn == 2)
+    def _():
+        pair(part, 0)
+
+    @pl.when(turn == 3)
+    def _():
+        give(part, 1)
+
+    @pl.when((turn == 3) & (part >= 2))
     def _():
         for copy in out(part - 2, lax.rem(part - 2, SLOTS)):
             copy.wait()
 
-    @pl.when(r == 3)
-    def _():
-        give(part)
-
     @pl.when(t == STEPS - 1)
     def _():
-        pair(part)
+        pair(part, 1)
         finish(part - 1)
         finish(part)
+        for n, peer in enumerate((core_peer, x_peer)):
+            copy = remote(sq.at[2 * n], sq.at[2 * n + 1], sq_send.at[n], sq_recv.at[n], peer)
+            copy.start()
+            copy.wait()
+            if n == 0:
+                sq[2] = sq[0] + sq[1]
+            else:
+                squares[...] = sq[2] + sq[3]
         for p in (part - 1, part):
             for copy in out(p, lax.rem(p, SLOTS)):
                 copy.wait()
@@ -317,20 +344,24 @@
         backward_kernel,
         grid=(STEPS,),
         in_specs=[pl.BlockSpec(memory_space=pl.ANY)] * 10,
-        out_specs=[pl.BlockSpec(memory_space=pl.ANY)] * 2 + [pl.BlockSpec((1, D), lambda t: (0, 0))],
+        out_specs=[pl.BlockSpec(memory_space=pl.ANY)] * 2 + [pl.BlockSpec((8, D), lambda t: (0, 0))],
         out_shape=[
             jax.ShapeDtypeStruct((LAYERS * PARTS, 2, ROWS, wide), BF16),
             jax.ShapeDtypeStruct((LAYERS * PARTS, SIZE, D), BF16),
-            jax.ShapeDtypeStruct((1, D), F32),
+            jax.ShapeDtypeStruct((8, D), F32),
         ],
         scratch_shapes=[
             *(vm(shape, BF16) for shape in (row, col, row, col, row)),
             vm(row, F32),
             *(vm(shape, BF16) for shape in ((2, D, 2 * SIZE), (2, SIZE, D), (TOKENS, SIZE), (TOKENS, 2 * SIZE), (SIZE, D), (D, 2 * SIZE))),
             *(vm(shape, BF16) for shape in (gu, gu, two_gu, two_gu, gu, d, d, two_d, two_d, d)),
+            vm((4, 8, D), F32),
             dma((2, 3)),
             dma((5,)),
-            *[dma((SLOTS, 2))] * 5,
+            *[dma((SLOTS, 2, 2))] * 4,
+            dma((SLOTS, 2)),
+            dma((2,)),
+            dma((2,)),
             pltpu.SemaphoreType.REGULAR,
             pltpu.SemaphoreType.REGULAR,
         ],
@@ -344,7 +375,7 @@
 
 def adamw_kernel(me_ref, f_ref, ggu, gd, wg, wu, wd, mg, mu, md, vg, vu, vd, *refs):
     ngu, nd, *mv = refs[-8:]
-    factor = f_ref[0, 0]
+    factor = jnp.minimum(1.0, 0.5 * lax.rsqrt(jnp.sum(f_ref[...], keepdims=True) / COUNT + 1e-30))
     for k, (g, w, m, v, to) in enumerate(
         (
             (jnp.concatenate([ggu[p, 0] for p in range(ggu.shape[0])], 1), wg.at[0], mg.at[0], vg.at[0], ngu.at[0]),
@@ -361,7 +392,7 @@
         mv[3 + k][0] = v
 
 
-def adamw(chunk, me, factor, ggu, gd, weights, m, v, so_far):
+def adamw(chunk, me, squares, ggu, gd, weights, m, v, so_far):
     layer, start, size = chunk
     step = size // DP
     w_spec = pl.BlockSpec((1, ROWS, size), lambda o, me: (layer, me[0], (o * OWN + start) // size))
@@ -379,7 +410,7 @@
         grid_spec=pltpu.PrefetchScalarGridSpec(
             num_scalar_prefetch=1,
             grid=(DP,),
-            in_specs=[pl.BlockSpec(memory_space=pltpu.SMEM), ggu_spec, gd_spec, w_spec, w_spec, wd_spec, *mv_specs]
+            in_specs=[whole((8, D)), ggu_spec, gd_spec, w_spec, w_spec, wd_spec, *mv_specs]
             + [pl.BlockSpec(memory_space=pl.ANY)] * len(so_far),
             out_specs=[gu_spec, d_spec, *mv_specs],
         ),
@@ -389,12 +420,12 @@
         compiler_params=params(1),
         cost_estimate=cost(0.25, 17e6),
         name="adamw",
-    )(me, factor, ggu, gd, *weights, *m, *v, *so_far)
-
-
-def assemble_kernel(me_ref, gu0, d0, gu1, d1, *refs):
+    )(me, squares, ggu, gd, *weights, *m, *v, *so_far)
+
+
+def assemble_kernel(owners, me_ref, *refs):
     wg, wu, wd = refs[-3:]
-    for q, (gu, d) in enumerate(((gu0, d0), (gu1, d1))):
+    for q, (gu, d) in enumerate(zip(refs[0 : 2 * owners : 2], refs[1 : 2 * owners : 2])):
 
         @pl.when(pl.program_id(0) == q)
         def _(gu=gu, d=d):
@@ -403,7 +434,7 @@
             wd[0] = d[...]
 
 
-def assemble(chunk, base, me, first, second, so_far):
+def assemble(chunk, base, me, blocks, so_far):
     layer, start, size = chunk
     step = size // DP
 
@@ -423,19 +454,19 @@
     wd_spec = pl.BlockSpec((1, step, D), lambda r, o, me: (layer, (owner(r, me) * OWN + start) // step + o, 0))
     wide, tall = jax.ShapeDtypeStruct((LAYERS, D, FF), BF16), jax.ShapeDtypeStruct((LAYERS, FF, D), BF16)
     return pl.pallas_call(
-        assemble_kernel,
+        functools.partial(assemble_kernel, len(blocks)),
         grid_spec=pltpu.PrefetchScalarGridSpec(
             num_scalar_prefetch=1,
-            grid=(2, DP),
-            in_specs=[gu_spec(0), d_spec(0), gu_spec(1), d_spec(1)] + [pl.BlockSpec(memory_space=pl.ANY)] * len(so_far),
+            grid=(len(blocks), DP),
+            in_specs=[spec(q) for q in range(len(blocks)) for spec in (gu_spec, d_spec)] + [pl.BlockSpec(memory_space=pl.ANY)] * len(so_far),
             out_specs=[w_spec, w_spec, wd_spec],
         ),
         out_shape=[wide, wide, tall],
-        input_output_aliases={5 + n: n for n in range(len(so_far))},
+        input_output_aliases={1 + 2 * len(blocks) + n: n for n in range(len(so_far))},
         compiler_params=params(2),
         cost_estimate=cost(0.15, 6e6),
         name="assemble",
-    )(me, *first, *second, *so_far)
+    )(me, *(t for block in blocks for t in block), *so_far)
 
 
 def to_core(t):
@@ -456,13 +487,11 @@
 
         gu, d, squares = backward(h1, a0, a0t, a1, a1t, dy, dyt, *weights)
         d = d.reshape(-1, D)
-        total = lax.psum(jnp.sum(squares), "dp")
-        factor = jnp.minimum(1.0, 0.5 * lax.rsqrt(total / COUNT + 1e-30)).reshape(1, 1)
 
         moments, own, near, far, last, new = (), {}, {}, {}, {}, ()
         turn = [LAST - 1, *range(LAST - 1), LAST]
         for n, k in enumerate(turn):
-            own_gu, own_d, *moments = adamw(CHUNKS[k], me, factor, gu, d, weights, m, v, moments)
+            own_gu, own_d, *moments = adamw(CHUNKS[k], me, squares, gu, d, weights, m, v, moments)
             own[n] = own_gu, own_d
             far[n] = tuple(map(to_x, own[n]))
             near[n] = tuple(map(to_core, own[n]))
@@ -470,8 +499,9 @@
         for n in range(LAST + 1):
             for ahead in (0, 1, 2) if n == 0 else (n + 2,):
                 if ahead <= LAST:
-                    new = assemble(CHUNKS[turn[ahead]], 0, me, own[ahead], near[ahead], new)
-            new = assemble(CHUNKS[turn[n]], 2, me, far[n], last[n], new)
+                    new = assemble(CHUNKS[turn[ahead]], 0, me, (own[ahead], near[ahead]), new)
+            for base, blocks in ((2, (far[n],)), (3, (last[n],))) if n == LAST else ((2, (far[n], last[n])),):
+                new = assemble(CHUNKS[turn[n]], base, me, blocks, new)
         return (*new, *moments)
 
     rows = P(None, "dp", None)

time: 779 us -> 773 us (level)
  waiting for transfers between devices: 158 us -> 175 us
  starting transfers between devices: 27.2 us -> 14.6 us
    ppermute x18, waiting for transfers between devices: 157 us -> 174 us  [to_x(): return lax.ppermute(t, 'dp', [(0, 2), (2, 0), (1, 3), (3, 1)])]
    ppermute x18, starting transfers between devices: 22 us -> 8.47 us  [to_x(): return lax.ppermute(t, 'dp', [(0, 2), (2, 0), (1, 3), (3, 1)])]
    pallas_call x18 -> x19, Pallas kernels: 112 us -> 113 us  [assemble(): pl.pallas_call(functools.partial(assemble_kernel, len(blocks)), grid_spec...]
  transfers between devices with their start and end apart: 54 -> 54, of which waited for: 15 -> 18; matrix products, arithmetic and copies ran while one was open for 0% -> 0% of each run, Pallas kernels for 21% -> 22%
where the time goes in v1:
time: 773 us; the launch traced here: 771 us
  Pallas kernels  568 us (73%)
  waiting for transfers between devices  175 us (23%)
  starting transfers between devices  14.6 us (2%)
  local copies, waits for them, and re-layouts  11.7 us (2%)
    pallas_call x1, Pallas kernels, backward(): pl.pallas_call(backward_kernel, grid=(STEPS,), in_specs=[pl.BlockSpec(mem...  322 us
    ppermute x18, waiting for transfers between devices, to_x(): return lax.ppermute(t, 'dp', [(0, 2), (2, 0), (1, 3), (3, 1)])  174 us
    pallas_call x19, Pallas kernels, assemble(): pl.pallas_call(functools.partial(assemble_kernel, len(blocks)), grid_spec...  113 us
    pallas_call x9, Pallas kernels, adamw(): pl.pallas_call(adamw_kernel, grid_spec=pltpu.PrefetchScalarGridSpec(num_s...  67.2 us
    pallas_call x1, Pallas kernels, forward(): pl.pallas_call(forward_kernel, grid=(FF // FT, TOKENS // FI), in_specs=[w...  66.5 us
  transfers between devices with their start and end apart: 54, of which 18 were waited for; matrix products, arithmetic and copies ran while one was open for 0% of the time, Pallas kernels for 22%

profile of v1, /device:TPU:0, one launch (start us, length us, event | category | flops | bytes accessed | tf_op | source)
XLA Modules:
  0.0 770.8 jit_solution(10558943805914485339)
XLA Ops:
  0.6 66.5 %forward0.1 = (bf16[2048,512]{1,0:T(8,128)(2,1)}, bf16[2048,512]{1,0:T(8,128)(2,1)}, bf16[2048,512]{1,0:T(8,128)(2,1)}, bf16[512,2048]{1,0:T(8,128)(2,1)}, bf16[...) custom-call(bf16[2048,512]{1,0:T(8,128)(2,1)} %bitcast.13, bf16[2048,512]{1,0:T(8,128)(2,1)} %bitcast.14, ...), custom_call_target="tpu_custom_call" | custom-call | flops 51539607552 | bytes 40000000 | tf_op jit(solution)/shard_map/forward0/pallas_call | solution.py:92
  67.1 321.9 %backward.1 = (bf16[16,2,128,1024]{3,2,1,0:T(8,128)(2,1)}, bf16[16,256,512]{2,1,0:T(8,128)(2,1)}, f32[8,512]{1,0:T(8,128)}) custom-call(bf16[2048,512]{1,0:T(8,128)(2,1)} %get-tuple-element.147.h1, bf16[2048,512]{1,0:T(8,128)(2,1)} %get-tuple-element.148.a0, bf16[512,2048]{1,0:T(8,128)(2,1)} %get-tuple-element.149.a0t, ...), custom_call_target="tpu_custom_call" | custom-call | flops 240518168576 | bytes 120000000 | tf_op jit(solution)/shard_map/backward/pallas_call | solution.py:343
  389.0 5.6 adamw.9
  394.6 2.3 collective-permute-start.45
  396.9 7.9 %adamw.10 = (bf16[2,128,2048]{2,1,0:T(8,128)(2,1)}, bf16[512,512]{1,0:T(8,128)(2,1)}, f32[2,128,8192]{2,1,0:T(8,128)}, f32[2,128,8192]{2,1,0:T(8,128)}, f32[2,20...) custom-call(s32[1]{0:T(128)} %bitcast.me_ref, ...), custom_call_target="tpu_custom_call", output_to_operand_aliasing={{2}: (13, {}), {3}: (14, {}), {4}: (15, {}), {5}: (16, {}),... | custom-call | flops 4294967296 | bytes 17000000 | tf_op jit(solution)/shard_map/adamw/pallas_call | solution.py:408
  404.8 7.9 %adamw.11 = (bf16[2,128,2048]{2,1,0:T(8,128)(2,1)}, bf16[512,512]{1,0:T(8,128)(2,1)}, f32[2,128,8192]{2,1,0:T(8,128)}, f32[2,128,8192]{2,1,0:T(8,128)}, f32[2,20...) custom-call(s32[1]{0:T(128)} %bitcast.me_ref, ...), custom_call_target="tpu_custom_call", output_to_operand_aliasing={{2}: (13, {}), {3}: (14, {}), {4}: (15, {}), {5}: (16, {}),... | custom-call | flops 4294967296 | bytes 17000000 | tf_op jit(solution)/shard_map/adamw/pallas_call | solution.py:408
  412.7 7.9 %adamw.12 = (bf16[2,128,2048]{2,1,0:T(8,128)(2,1)}, bf16[512,512]{1,0:T(8,128)(2,1)}, f32[2,128,8192]{2,1,0:T(8,128)}, f32[2,128,8192]{2,1,0:T(8,128)}, f32[2,20...) custom-call(s32[1]{0:T(128)} %bitcast.me_ref, ...), custom_call_target="tpu_custom_call", output_to_operand_aliasing={{2}: (13, {}), {3}: (14, {}), {4}: (15, {}), {5}: (16, {}),... | custom-call | flops 4294967296 | bytes 17000000 | tf_op jit(solution)/shard_map/adamw/pallas_call | solution.py:408
  420.7 7.9 %adamw.13 = (bf16[2,128,2048]{2,1,0:T(8,128)(2,1)}, bf16[512,512]{1,0:T(8,128)(2,1)}, f32[2,128,8192]{2,1,0:T(8,128)}, f32[2,128,8192]{2,1,0:T(8,128)}, f32[2,20...) custom-call(s32[1]{0:T(128)} %bitcast.me_ref, ...), custom_call_target="tpu_custom_call", output_to_operand_aliasing={{2}: (13, {}), {3}: (14, {}), {4}: (15, {}), {5}: (16, {}),... | custom-call | flops 4294967296 | bytes 17000000 | tf_op jit(solution)/shard_map/adamw/pallas_call | solution.py:408
  428.6 8.0 %adamw.14 = (bf16[2,128,2048]{2,1,0:T(8,128)(2,1)}, bf16[512,512]{1,0:T(8,128)(2,1)}, f32[2,128,8192]{2,1,0:T(8,128)}, f32[2,128,8192]{2,1,0:T(8,128)}, f32[2,20...) custom-call(s32[1]{0:T(128)} %bitcast.me_ref, ...), custom_call_target="tpu_custom_call", output_to_operand_aliasing={{2}: (13, {}), {3}: (14, {}), {4}: (15, {}), {5}: (16, {}),... | custom-call | flops 4294967296 | bytes 17000000 | tf_op jit(solution)/shard_map/adamw/pallas_call | solution.py:408
  436.7 8.1 %adamw.15 = (bf16[2,128,2048]{2,1,0:T(8,128)(2,1)}, bf16[512,512]{1,0:T(8,128)(2,1)}, f32[2,128,8192]{2,1,0:T(8,128)}, f32[2,128,8192]{2,1,0:T(8,128)}, f32[2,20...) custom-call(s32[1]{0:T(128)} %bitcast.me_ref, ...), custom_call_target="tpu_custom_call", output_to_operand_aliasing={{2}: (13, {}), {3}: (14, {}), {4}: (15, {}), {5}: (16, {}),... | custom-call | flops 4294967296 | bytes 17000000 | tf_op jit(solution)/shard_map/adamw/pallas_call | solution.py:408
  444.8 8.1 %adamw.16 = (bf16[2,128,2048]{2,1,0:T(8,128)(2,1)}, bf16[512,512]{1,0:T(8,128)(2,1)}, f32[2,128,8192]{2,1,0:T(8,128)}, f32[2,128,8192]{2,1,0:T(8,128)}, f32[2,20...) custom-call(s32[1]{0:T(128)} %bitcast.me_ref, ...), custom_call_target="tpu_custom_call", output_to_operand_aliasing={{2}: (13, {}), {3}: (14, {}), {4}: (15, {}), {5}: (16, {}),... | custom-call | flops 4294967296 | bytes 17000000 | tf_op jit(solution)/shard_map/adamw/pallas_call | solution.py:408
  453.0 5.6 adamw.17
  461.7 7.4 collective-permute-done.2.refs_1_
  471.3 9.0 %collective-permute-done.44.refs_0_ = bf16[2,128,1024]{2,1,0:T(8,128)(2,1)S(1)} collective-permute-done((bf16[2,128,1024]{2,1,0:T(8,128)(2,1)}, bf16[2,128,1024]{2,1,0:T(8,128)(2,1)S(1)}, u32[]{:S(2)}, u32[]{:S(2)}) %collective-permute-start.44) | collective-permute-done | bytes 524320 | tf_op jit(solution)/shard_map/ppermute | solution.py:477
  480.4 2.0 collective-permute-start.27
  482.4 9.1 %collective-permute-done.39.refs_1_ = bf16[512,512]{1,0:T(8,128)(2,1)S(1)} collective-permute-done((bf16[512,512]{1,0:T(8,128)(2,1)}, bf16[512,512]{1,0:T(8,128)(2,1)S(1)}, u32[]{:S(2)}, u32[]{:S(2)}) %collective-permute-start.39) | collective-permute-done | bytes 524320 | tf_op jit(solution)/shard_map/ppermute | solution.py:477
  491.6 11.1 %collective-permute-done.33.refs_1_ = bf16[512,512]{1,0:T(8,128)(2,1)S(1)} collective-permute-done((bf16[512,512]{1,0:T(8,128)(2,1)}, bf16[512,512]{1,0:T(8,128)(2,1)S(1)}, u32[]{:S(2)}, u32[]{:S(2)}) %collective-permute-start.33) | collective-permute-done | bytes 524320 | tf_op jit(solution)/shard_map/ppermute | solution.py:477
  502.9 11.2 %collective-permute-done.27.refs_1_ = bf16[512,512]{1,0:T(8,128)(2,1)} collective-permute-done((bf16[512,512]{1,0:T(8,128)(2,1)}, bf16[512,512]{1,0:T(8,128)(2,1)}, u32[]{:S(2)}, u32[]{:S(2)}) %collective-permute-start.27) | collective-permute-done | bytes 524320 | tf_op jit(solution)/shard_map/ppermute | solution.py:477
  515.4 9.8 %collective-permute-done.21.refs_1_ = bf16[512,512]{1,0:T(8,128)(2,1)S(1)} collective-permute-done((bf16[512,512]{1,0:T(8,128)(2,1)}, bf16[512,512]{1,0:T(8,128)(2,1)S(1)}, u32[]{:S(2)}, u32[]{:S(2)}) %collective-permute-start.21) | collective-permute-done | bytes 524320 | tf_op jit(solution)/shard_map/ppermute | solution.py:477
  526.0 10.5 %collective-permute-done.15.refs_1_ = bf16[512,512]{1,0:T(8,128)(2,1)} collective-permute-done((bf16[512,512]{1,0:T(8,128)(2,1)}, bf16[512,512]{1,0:T(8,128)(2,1)}, u32[]{:S(2)}, u32[]{:S(2)}) %collective-permute-start.15) | collective-permute-done | bytes 524320 | tf_op jit(solution)/shard_map/ppermute | solution.py:477
  537.4 10.3 %collective-permute-done.9.refs_1_ = bf16[512,512]{1,0:T(8,128)(2,1)S(1)} collective-permute-done((bf16[512,512]{1,0:T(8,128)(2,1)}, bf16[512,512]{1,0:T(8,128)(2,1)S(1)}, u32[]{:S(2)}, u32[]{:S(2)}) %collective-permute-start.9) | collective-permute-done | bytes 524320 | tf_op jit(solution)/shard_map/ppermute | solution.py:477
  547.7 11.2 %collective-permute-done.5.refs_1_ = bf16[512,512]{1,0:T(8,128)(2,1)S(1)} collective-permute-done((bf16[512,512]{1,0:T(8,128)(2,1)S(1)}, bf16[512,512]{1,0:T(8,128)(2,1)S(1)}, u32[]{:S(2)}, u32[]{:S(2)}) %collective-permute-start.5) | collective-permute-done | bytes 524320 | tf_op jit(solution)/shard_map/ppermute | solution.py:477
  562.4 19.1 %collective-permute-done.38.refs_0_ = bf16[2,128,2048]{2,1,0:T(8,128)(2,1)} collective-permute-done((bf16[2,128,2048]{2,1,0:T(8,128)(2,1)}, bf16[2,128,2048]{2,1,0:T(8,128)(2,1)}, u32[]{:S(2)}, u32[]{:S(2)}) %collective-permute-start.38) | collective-permute-done | bytes 1048608 | tf_op jit(solution)/shard_map/ppermute | solution.py:477
  582.1 21.8 %collective-permute-done.32.refs_0_ = bf16[2,128,2048]{2,1,0:T(8,128)(2,1)S(1)} collective-permute-done((bf16[2,128,2048]{2,1,0:T(8,128)(2,1)}, bf16[2,128,2048]{2,1,0:T(8,128)(2,1)S(1)}, u32[]{:S(2)}, u32[]{:S(2)}) %collective-permute-start.32) | collective-permute-done | bytes 1048608 | tf_op jit(solution)/shard_map/ppermute | solution.py:477
  606.1 5.6 assemble.19
  611.7 14.8 %collective-permute-done.26.refs_0_ = bf16[2,128,2048]{2,1,0:T(8,128)(2,1)} collective-permute-done((bf16[2,128,2048]{2,1,0:T(8,128)(2,1)}, bf16[2,128,2048]{2,1,0:T(8,128)(2,1)}, u32[]{:S(2)}, u32[]{:S(2)}) %collective-permute-start.26) | collective-permute-done | bytes 1048608 | tf_op jit(solution)/shard_map/ppermute | solution.py:477
  626.5 6.4 assemble.20
  633.4 6.4 assemble.21
  639.8 9.1 %collective-permute-done.20.refs_0_ = bf16[2,128,2048]{2,1,0:T(8,128)(2,1)} collective-permute-done((bf16[2,128,2048]{2,1,0:T(8,128)(2,1)S(1)}, bf16[2,128,2048]{2,1,0:T(8,128)(2,1)}, u32[]{:S(2)}, u32[]{:S(2)}) %collective-permute-start.20) | collective-permute-done | bytes 1048608 | tf_op jit(solution)/shard_map/ppermute | solution.py:477
  649.0 5.5 assemble.22
  654.6 6.5 assemble.23
  661.1 2.0 collective-permute-start.4
  663.1 6.4 assemble.24
  671.4 6.4 assemble.25
  678.3 6.4 assemble.26
  684.7 9.2 %collective-permute-done.8.refs_0_ = bf16[2,128,2048]{2,1,0:T(8,128)(2,1)} collective-permute-done((bf16[2,128,2048]{2,1,0:T(8,128)(2,1)S(1)}, bf16[2,128,2048]{2,1,0:T(8,128)(2,1)}, u32[]{:S(2)}, u32[]{:S(2)}) %collective-permute-start.8) | collective-permute-done | bytes 1048608 | tf_op jit(solution)/shard_map/ppermute | solution.py:477
  693.9 6.4 assemble.27
  700.8 6.4 assemble.28
  707.1 8.4 %collective-permute-done.4.refs_0_ = bf16[2,128,2048]{2,1,0:T(8,128)(2,1)} collective-permute-done((bf16[2,128,2048]{2,1,0:T(8,128)(2,1)S(1)}, bf16[2,128,2048]{2,1,0:T(8,128)(2,1)}, u32[]{:S(2)}, u32[]{:S(2)}) %collective-permute-start.4) | collective-permute-done | bytes 1048608 | tf_op jit(solution)/shard_map/ppermute | solution.py:477
  715.6 6.4 assemble.29
  722.5 6.4 assemble.30
  729.2 6.5 assemble.31
  736.2 6.4 assemble.32
  742.6 5.6 assemble.33
  749.8 6.4 assemble.34
  757.2 6.4 assemble.35
  763.6 3.2 assemble.36
  767.6 3.2 assemble.37
  (166 shorter events, 22.8 us)
Async XLA Ops:
  394.5 64.8 %collective-permute-start.53 = (bf16[256,512]{1,0:T(8,128)(2,1)}, bf16[256,512]{1,0:T(8,128)(2,1)}, u32[]{:S(2)}, u32[]{:S(2)}) collective-permute-start(bf16[256,512]{1,0:T(8,128)(2,1)} %get-tuple-element.221.refs_1_), channel_id=1, source_target_pairs={{0,1},{1,0},{2,3},{3,2},{4,5},{5,4},{6,7},{7,6}} | collective-permute-start | bytes 786440 | tf_op jit(solution)/shard_map/ppermute | solution.py:473
  394.6 65.1 %collective-permute-start.45 = (bf16[256,512]{1,0:T(8,128)(2,1)}, bf16[256,512]{1,0:T(8,128)(2,1)}, u32[]{:S(2)}, u32[]{:S(2)}) collective-permute-start(bf16[256,512]{1,0:T(8,128)(2,1)} %get-tuple-element.221.refs_1_), channel_id=1, source_target_pairs={{0,2},{2,0},{1,3},{3,1},{4,6},{6,4},{5,7},{7,5}} | collective-permute-start | bytes 786440 | tf_op jit(solution)/shard_map/ppermute | solution.py:477
  459.1 11.2 %collective-permute-start.51 = (bf16[512,512]{1,0:T(8,128)(2,1)}, bf16[512,512]{1,0:T(8,128)(2,1)S(1)}, u32[]{:S(2)}, u32[]{:S(2)}) collective-permute-start(bf16[512,512]{1,0:T(8,128)(2,1)} %get-tuple-element.219.refs_1_), channel_id=1, source_target_pairs={{0,1},{1,0},{2,3},{3,2},{4,5},{5,4},{6,7},{7,6}} | collective-permute-start | bytes 1572872 | tf_op jit(solution)/shard_map/ppermute | solution.py:473
  459.3 11.0 %collective-permute-start.49 = (bf16[512,512]{1,0:T(8,128)(2,1)}, bf16[512,512]{1,0:T(8,128)(2,1)S(1)}, u32[]{:S(2)}, u32[]{:S(2)}) collective-permute-start(bf16[512,512]{1,0:T(8,128)(2,1)} %get-tuple-element.217.refs_1_), channel_id=1, source_target_pairs={{0,1},{1,0},{2,3},{3,2},{4,5},{5,4},{6,7},{7,6}} | collective-permute-start | bytes 1572872 | tf_op jit(solution)/shard_map/ppermute | solution.py:473
  460.4 19.9 %collective-permute-start.44 = (bf16[2,128,1024]{2,1,0:T(8,128)(2,1)}, bf16[2,128,1024]{2,1,0:T(8,128)(2,1)S(1)}, u32[]{:S(2)}, u32[]{:S(2)}) collective-permute-start(bf16[2,128,1024]{2,1,0:T(8,128)(2,1)} %get-tuple-element.220.refs_0_), channel_id=1, source_target_pairs={{0,2},{2,0},{1,3},{3,1},{4,6},{6,4},{5,7},{7,5}} | collective-permute-start | bytes 1572872 | tf_op jit(solution)/shard_map/ppermute | solution.py:477
  470.3 21.2 %collective-permute-start.39 = (bf16[512,512]{1,0:T(8,128)(2,1)}, bf16[512,512]{1,0:T(8,128)(2,1)S(1)}, u32[]{:S(2)}, u32[]{:S(2)}) collective-permute-start(bf16[512,512]{1,0:T(8,128)(2,1)} %get-tuple-element.219.refs_1_), channel_id=1, source_target_pairs={{0,2},{2,0},{1,3},{3,1},{4,6},{6,4},{5,7},{7,5}} | collective-permute-start | bytes 1572872 | tf_op jit(solution)/shard_map/ppermute | solution.py:477
  471.2 20.3 %collective-permute-start.37 = (bf16[512,512]{1,0:T(8,128)(2,1)}, bf16[512,512]{1,0:T(8,128)(2,1)S(1)}, u32[]{:S(2)}, u32[]{:S(2)}) collective-permute-start(bf16[512,512]{1,0:T(8,128)(2,1)} %get-tuple-element.213.refs_1_), channel_id=1, source_target_pairs={{0,1},{1,0},{2,3},{3,2},{4,5},{5,4},{6,7},{7,6}} | collective-permute-start | bytes 1572872 | tf_op jit(solution)/shard_map/ppermute | solution.py:473
  480.3 22.5 %collective-permute-start.33 = (bf16[512,512]{1,0:T(8,128)(2,1)}, bf16[512,512]{1,0:T(8,128)(2,1)S(1)}, u32[]{:S(2)}, u32[]{:S(2)}) collective-permute-start(bf16[512,512]{1,0:T(8,128)(2,1)} %get-tuple-element.217.refs_1_), channel_id=1, source_target_pairs={{0,2},{2,0},{1,3},{3,1},{4,6},{6,4},{5,7},{7,5}} | collective-permute-start | bytes 1572872 | tf_op jit(solution)/shard_map/ppermute | solution.py:477
  480.3 22.5 %collective-permute-start.31 = (bf16[512,512]{1,0:T(8,128)(2,1)}, bf16[512,512]{1,0:T(8,128)(2,1)S(1)}, u32[]{:S(2)}, u32[]{:S(2)}) collective-permute-start(bf16[512,512]{1,0:T(8,128)(2,1)} %get-tuple-element.211.refs_1_), channel_id=1, source_target_pairs={{0,1},{1,0},{2,3},{3,2},{4,5},{5,4},{6,7},{7,6}} | collective-permute-start | bytes 1572872 | tf_op jit(solution)/shard_map/ppermute | solution.py:473
  480.4 33.7 %collective-permute-start.27 = (bf16[512,512]{1,0:T(8,128)(2,1)}, bf16[512,512]{1,0:T(8,128)(2,1)}, u32[]{:S(2)}, u32[]{:S(2)}) collective-permute-start(bf16[512,512]{1,0:T(8,128)(2,1)} %get-tuple-element.215.refs_1_), channel_id=1, source_target_pairs={{0,2},{2,0},{1,3},{3,1},{4,6},{6,4},{5,7},{7,5}} | collective-permute-start | bytes 1572872 | tf_op jit(solution)/shard_map/ppermute | solution.py:477
  491.5 22.6 %collective-permute-start.25 = (bf16[512,512]{1,0:T(8,128)(2,1)}, bf16[512,512]{1,0:T(8,128)(2,1)S(1)}, u32[]{:S(2)}, u32[]{:S(2)}) collective-permute-start(bf16[512,512]{1,0:T(8,128)(2,1)} %get-tuple-element.209.refs_1_), channel_id=1, source_target_pairs={{0,1},{1,0},{2,3},{3,2},{4,5},{5,4},{6,7},{7,6}} | collective-permute-start | bytes 1572872 | tf_op jit(solution)/shard_map/ppermute | solution.py:473
  491.6 33.7 %collective-permute-start.21 = (bf16[512,512]{1,0:T(8,128)(2,1)}, bf16[512,512]{1,0:T(8,128)(2,1)S(1)}, u32[]{:S(2)}, u32[]{:S(2)}) collective-permute-start(bf16[512,512]{1,0:T(8,128)(2,1)} %get-tuple-element.213.refs_1_), channel_id=1, source_target_pairs={{0,2},{2,0},{1,3},{3,1},{4,6},{6,4},{5,7},{7,5}} | collective-permute-start | bytes 1572872 | tf_op jit(solution)/shard_map/ppermute | solution.py:477
  502.8 22.5 %collective-permute-start.19 = (bf16[512,512]{1,0:T(8,128)(2,1)S(1)}, bf16[512,512]{1,0:T(8,128)(2,1)S(1)}, u32[]{:S(2)}, u32[]{:S(2)}) collective-permute-start(bf16[512,512]{1,0:T(8,128)(2,1)S(1)} %copy-done.12), channel_id=1, source_target_pairs={{0,1},{1,0},{2,3},{3,2},{4,5},{5,4},{6,7},{7,6}} | collective-permute-start | bytes 1572872 | tf_op jit(solution)/shard_map/ppermute | solution.py:473
  502.8 33.8 %collective-permute-start.15 = (bf16[512,512]{1,0:T(8,128)(2,1)}, bf16[512,512]{1,0:T(8,128)(2,1)}, u32[]{:S(2)}, u32[]{:S(2)}) collective-permute-start(bf16[512,512]{1,0:T(8,128)(2,1)} %get-tuple-element.211.refs_1_), channel_id=1, source_target_pairs={{0,2},{2,0},{1,3},{3,1},{4,6},{6,4},{5,7},{7,5}} | collective-permute-start | bytes 1572872 | tf_op jit(solution)/shard_map/ppermute | solution.py:477
  514.1 44.8 %collective-permute-start.50 = (bf16[2,128,2048]{2,1,0:T(8,128)(2,1)}, bf16[2,128,2048]{2,1,0:T(8,128)(2,1)S(1)}, u32[]{:S(2)}, u32[]{:S(2)}) collective-permute-start(bf16[2,128,2048]{2,1,0:T(8,128)(2,1)} %get-tuple-element.218.refs_0_), channel_id=1, source_target_pairs={{0,1},{1,0},{2,3},{3,2},{4,5},{5,4},{6,7},{7,6}} | collective-permute-start | bytes 3145736 | tf_op jit(solution)/shard_map/ppermute | solution.py:473
  514.9 21.7 %collective-permute-start.12 = (bf16[2,128,1024]{2,1,0:T(8,128)(2,1)}, bf16[2,128,1024]{2,1,0:T(8,128)(2,1)S(1)}, u32[]{:S(2)}, u32[]{:S(2)}) collective-permute-start(bf16[2,128,1024]{2,1,0:T(8,128)(2,1)} %get-tuple-element.204.refs_0_), channel_id=1, source_target_pairs={{0,1},{1,0},{2,3},{3,2},{4,5},{5,4},{6,7},{7,6}} | collective-permute-start | bytes 1572872 | tf_op jit(solution)/shard_map/ppermute | solution.py:473
  525.2 35.5 %collective-permute-start.48 = (bf16[2,128,2048]{2,1,0:T(8,128)(2,1)}, bf16[2,128,2048]{2,1,0:T(8,128)(2,1)}, u32[]{:S(2)}, u32[]{:S(2)}) collective-permute-start(bf16[2,128,2048]{2,1,0:T(8,128)(2,1)} %get-tuple-element.216.refs_0_), channel_id=1, source_target_pairs={{0,1},{1,0},{2,3},{3,2},{4,5},{5,4},{6,7},{7,6}} | collective-permute-start | bytes 3145736 | tf_op jit(solution)/shard_map/ppermute | solution.py:473
  525.3 22.4 %collective-permute-start.9 = (bf16[512,512]{1,0:T(8,128)(2,1)}, bf16[512,512]{1,0:T(8,128)(2,1)S(1)}, u32[]{:S(2)}, u32[]{:S(2)}) collective-permute-start(bf16[512,512]{1,0:T(8,128)(2,1)} %get-tuple-element.209.refs_1_), channel_id=1, source_target_pairs={{0,2},{2,0},{1,3},{3,1},{4,6},{6,4},{5,7},{7,5}} | collective-permute-start | bytes 1572872 | tf_op jit(solution)/shard_map/ppermute | solution.py:477
  536.6 22.4 %collective-permute-start.5 = (bf16[512,512]{1,0:T(8,128)(2,1)S(1)}, bf16[512,512]{1,0:T(8,128)(2,1)S(1)}, u32[]{:S(2)}, u32[]{:S(2)}) collective-permute-start(bf16[512,512]{1,0:T(8,128)(2,1)S(1)} %copy-done.12), channel_id=1, source_target_pairs={{0,2},{2,0},{1,3},{3,1},{4,6},{6,4},{5,7},{7,5}} | collective-permute-start | bytes 1572872 | tf_op jit(solution)/shard_map/ppermute | solution.py:477
  537.4 23.6 %collective-permute-start.42 = (bf16[2,128,2048]{2,1,0:T(8,128)(2,1)}, bf16[2,128,2048]{2,1,0:T(8,128)(2,1)S(1)}, u32[]{:S(2)}, u32[]{:S(2)}) collective-permute-start(bf16[2,128,2048]{2,1,0:T(8,128)(2,1)} %get-tuple-element.214.refs_0_), channel_id=1, source_target_pairs={{0,1},{1,0},{2,3},{3,2},{4,5},{5,4},{6,7},{7,6}} | collective-permute-start | bytes 3145736 | tf_op jit(solution)/shard_map/ppermute | solution.py:473
  547.7 33.8 %collective-permute-start.38 = (bf16[2,128,2048]{2,1,0:T(8,128)(2,1)}, bf16[2,128,2048]{2,1,0:T(8,128)(2,1)}, u32[]{:S(2)}, u32[]{:S(2)}) collective-permute-start(bf16[2,128,2048]{2,1,0:T(8,128)(2,1)} %get-tuple-element.218.refs_0_), channel_id=1, source_target_pairs={{0,2},{2,0},{1,3},{3,1},{4,6},{6,4},{5,7},{7,5}} | collective-permute-start | bytes 3145736 | tf_op jit(solution)/shard_map/ppermute | solution.py:477
  559.8 21.8 %collective-permute-start.36 = (bf16[2,128,2048]{2,1,0:T(8,128)(2,1)S(1)}, bf16[2,128,2048]{2,1,0:T(8,128)(2,1)S(1)}, u32[]{:S(2)}, u32[]{:S(2)}) collective-permute-start(bf16[2,128,2048]{2,1,0:T(8,128)(2,1)S(1)} %copy-done.3), channel_id=1, source_target_pairs={{0,1},{1,0},{2,3},{3,2},{4,5},{5,4},{6,7},{7,6}} | collective-permute-start | bytes 3145736 | tf_op jit(solution)/shard_map/ppermute | solution.py:473
  560.7 43.1 %collective-permute-start.32 = (bf16[2,128,2048]{2,1,0:T(8,128)(2,1)}, bf16[2,128,2048]{2,1,0:T(8,128)(2,1)S(1)}, u32[]{:S(2)}, u32[]{:S(2)}) collective-permute-start(bf16[2,128,2048]{2,1,0:T(8,128)(2,1)} %get-tuple-element.216.refs_0_), channel_id=1, source_target_pairs={{0,2},{2,0},{1,3},{3,1},{4,6},{6,4},{5,7},{7,5}} | collective-permute-start | bytes 3145736 | tf_op jit(solution)/shard_map/ppermute | solution.py:477
  560.9 20.7 %collective-permute-start.41 = (bf16[512,512]{1,0:T(8,128)(2,1)S(1)}, bf16[512,512]{1,0:T(8,128)(2,1)}, u32[]{:S(2)}, u32[]{:S(2)}) collective-permute-start(bf16[512,512]{1,0:T(8,128)(2,1)S(1)} %collective-permute-done.39.refs_1_), channel_id=1, source_target_pairs={{0,1},{1,0},{2,3},{3,2},{4,5},{5,4},{6,7},{7,6}} | collective-permute-start | bytes 1572872 | tf_op jit(solution)/shard_map/ppermute | solution.py:473
  562.0 41.9 %collective-permute-start.30 = (bf16[2,128,2048]{2,1,0:T(8,128)(2,1)S(1)}, bf16[2,128,2048]{2,1,0:T(8,128)(2,1)S(1)}, u32[]{:S(2)}, u32[]{:S(2)}) collective-permute-start(bf16[2,128,2048]{2,1,0:T(8,128)(2,1)S(1)} %copy-done.2), channel_id=1, source_target_pairs={{0,1},{1,0},{2,3},{3,2},{4,5},{5,4},{6,7},{7,6}} | collective-permute-start | bytes 3145736 | tf_op jit(solution)/shard_map/ppermute | solution.py:473
  581.5 44.9 %collective-permute-start.26 = (bf16[2,128,2048]{2,1,0:T(8,128)(2,1)}, bf16[2,128,2048]{2,1,0:T(8,128)(2,1)}, u32[]{:S(2)}, u32[]{:S(2)}) collective-permute-start(bf16[2,128,2048]{2,1,0:T(8,128)(2,1)} %get-tuple-element.214.refs_0_), channel_id=1, source_target_pairs={{0,2},{2,0},{1,3},{3,1},{4,6},{6,4},{5,7},{7,5}} | collective-permute-start | bytes 3145736 | tf_op jit(solution)/shard_map/ppermute | solution.py:477
  581.6 22.4 %collective-permute-start.35 = (bf16[512,512]{1,0:T(8,128)(2,1)S(1)}, bf16[512,512]{1,0:T(8,128)(2,1)S(1)}, u32[]{:S(2)}, u32[]{:S(2)}) collective-permute-start(bf16[512,512]{1,0:T(8,128)(2,1)S(1)} %collective-permute-done.33.refs_1_), channel_id=1, source_target_pairs={{0,1},{1,0},{2,3},{3,2},{4,5},{5,4},{6,7},{7,6}} | collective-permute-start | bytes 1572872 | tf_op jit(solution)/shard_map/ppermute | solution.py:473
  581.6 51.4 %collective-permute-start.24 = (bf16[2,128,2048]{2,1,0:T(8,128)(2,1)S(1)}, bf16[2,128,2048]{2,1,0:T(8,128)(2,1)}, u32[]{:S(2)}, u32[]{:S(2)}) collective-permute-start(bf16[2,128,2048]{2,1,0:T(8,128)(2,1)S(1)} %copy-done.1), channel_id=1, source_target_pairs={{0,1},{1,0},{2,3},{3,2},{4,5},{5,4},{6,7},{7,6}} | collective-permute-start | bytes 3145736 | tf_op jit(solution)/shard_map/ppermute | solution.py:473
  603.9 45.0 %collective-permute-start.20 = (bf16[2,128,2048]{2,1,0:T(8,128)(2,1)S(1)}, bf16[2,128,2048]{2,1,0:T(8,128)(2,1)}, u32[]{:S(2)}, u32[]{:S(2)}) collective-permute-start(bf16[2,128,2048]{2,1,0:T(8,128)(2,1)S(1)} %copy-done.3), channel_id=1, source_target_pairs={{0,2},{2,0},{1,3},{3,1},{4,6},{6,4},{5,7},{7,5}} | collective-permute-start | bytes 3145736 | tf_op jit(solution)/shard_map/ppermute | solution.py:477
  603.9 22.6 %collective-permute-start.29 = (bf16[512,512]{1,0:T(8,128)(2,1)}, bf16[512,512]{1,0:T(8,128)(2,1)}, u32[]{:S(2)}, u32[]{:S(2)}) collective-permute-start(bf16[512,512]{1,0:T(8,128)(2,1)} %collective-permute-done.27.refs_1_), channel_id=1, source_target_pairs={{0,1},{1,0},{2,3},{3,2},{4,5},{5,4},{6,7},{7,6}} | collective-permute-start | bytes 1572872 | tf_op jit(solution)/shard_map/ppermute | solution.py:473
  606.1 55.0 %collective-permute-start.40 = (bf16[2,128,2048]{2,1,0:T(8,128)(2,1)}, bf16[2,128,2048]{2,1,0:T(8,128)(2,1)}, u32[]{:S(2)}, u32[]{:S(2)}) collective-permute-start(bf16[2,128,2048]{2,1,0:T(8,128)(2,1)} %collective-permute-done.38.refs_0_), channel_id=1, source_target_pairs={{0,1},{1,0},{2,3},{3,2},{4,5},{5,4},{6,7},{7,6}} | collective-permute-start | bytes 3145736 | tf_op jit(solution)/shard_map/ppermute | solution.py:473
  626.5 44.9 %collective-permute-start.14 = (bf16[2,128,2048]{2,1,0:T(8,128)(2,1)S(1)}, bf16[2,128,2048]{2,1,0:T(8,128)(2,1)}, u32[]{:S(2)}, u32[]{:S(2)}) collective-permute-start(bf16[2,128,2048]{2,1,0:T(8,128)(2,1)S(1)} %copy-done.2), channel_id=1, source_target_pairs={{0,2},{2,0},{1,3},{3,1},{4,6},{6,4},{5,7},{7,5}} | collective-permute-start | bytes 3145736 | tf_op jit(solution)/shard_map/ppermute | solution.py:477
  626.5 28.0 %collective-permute-start.23 = (bf16[512,512]{1,0:T(8,128)(2,1)S(1)}, bf16[512,512]{1,0:T(8,128)(2,1)}, u32[]{:S(2)}, u32[]{:S(2)}) collective-permute-start(bf16[512,512]{1,0:T(8,128)(2,1)S(1)} %copy-done.19), channel_id=1, source_target_pairs={{0,1},{1,0},{2,3},{3,2},{4,5},{5,4},{6,7},{7,6}} | collective-permute-start | bytes 1572872 | tf_op jit(solution)/shard_map/ppermute | solution.py:473
  633.0 44.9 %collective-permute-start.34 = (bf16[2,128,2048]{2,1,0:T(8,128)(2,1)}, bf16[2,128,2048]{2,1,0:T(8,128)(2,1)}, u32[]{:S(2)}, u32[]{:S(2)}) collective-permute-start(bf16[2,128,2048]{2,1,0:T(8,128)(2,1)} %copy-done.5), channel_id=1, source_target_pairs={{0,1},{1,0},{2,3},{3,2},{4,5},{5,4},{6,7},{7,6}} | collective-permute-start | bytes 3145736 | tf_op jit(solution)/shard_map/ppermute | solution.py:473
  648.9 44.9 %collective-permute-start.8 = (bf16[2,128,2048]{2,1,0:T(8,128)(2,1)S(1)}, bf16[2,128,2048]{2,1,0:T(8,128)(2,1)}, u32[]{:S(2)}, u32[]{:S(2)}) collective-permute-start(bf16[2,128,2048]{2,1,0:T(8,128)(2,1)S(1)} %copy-done.1), channel_id=1, source_target_pairs={{0,2},{2,0},{1,3},{3,1},{4,6},{6,4},{5,7},{7,5}} | collective-permute-start | bytes 3145736 | tf_op jit(solution)/shard_map/ppermute | solution.py:477
  654.5 45.8 %collective-permute-start.28 = (bf16[2,128,2048]{2,1,0:T(8,128)(2,1)}, bf16[2,128,2048]{2,1,0:T(8,128)(2,1)}, u32[]{:S(2)}, u32[]{:S(2)}) collective-permute-start(bf16[2,128,2048]{2,1,0:T(8,128)(2,1)} %collective-permute-done.26.refs_0_), channel_id=1, source_target_pairs={{0,1},{1,0},{2,3},{3,2},{4,5},{5,4},{6,7},{7,6}} | collective-permute-start | bytes 3145736 | tf_op jit(solution)/shard_map/ppermute | solution.py:473
  661.1 54.5 %collective-permute-start.4 = (bf16[2,128,2048]{2,1,0:T(8,128)(2,1)S(1)}, bf16[2,128,2048]{2,1,0:T(8,128)(2,1)}, u32[]{:S(2)}, u32[]{:S(2)}) collective-permute-start(bf16[2,128,2048]{2,1,0:T(8,128)(2,1)S(1)} %copy-done), channel_id=1, source_target_pairs={{0,2},{2,0},{1,3},{3,1},{4,6},{6,4},{5,7},{7,5}} | collective-permute-start | bytes 3145736 | tf_op jit(solution)/shard_map/ppermute | solution.py:477
  671.4 50.6 %collective-permute-start.22 = (bf16[2,128,2048]{2,1,0:T(8,128)(2,1)}, bf16[2,128,2048]{2,1,0:T(8,128)(2,1)}, u32[]{:S(2)}, u32[]{:S(2)}) collective-permute-start(bf16[2,128,2048]{2,1,0:T(8,128)(2,1)} %collective-permute-done.20.refs_0_), channel_id=1, source_target_pairs={{0,1},{1,0},{2,3},{3,2},{4,5},{5,4},{6,7},{7,6}} | collective-permute-start | bytes 3145736 | tf_op jit(solution)/shard_map/ppermute | solution.py:473
  677.8 51.1 %collective-permute-start.18 = (bf16[2,128,2048]{2,1,0:T(8,128)(2,1)S(1)}, bf16[2,128,2048]{2,1,0:T(8,128)(2,1)}, u32[]{:S(2)}, u32[]{:S(2)}) collective-permute-start(bf16[2,128,2048]{2,1,0:T(8,128)(2,1)S(1)} %copy-done), channel_id=1, source_target_pairs={{0,1},{1,0},{2,3},{3,2},{4,5},{5,4},{6,7},{7,6}} | collective-permute-start | bytes 3145736 | tf_op jit(solution)/shard_map/ppermute | solution.py:473
  693.9 41.8 %collective-permute-start.16 = (bf16[2,128,2048]{2,1,0:T(8,128)(2,1)}, bf16[2,128,2048]{2,1,0:T(8,128)(2,1)}, u32[]{:S(2)}, u32[]{:S(2)}) collective-permute-start(bf16[2,128,2048]{2,1,0:T(8,128)(2,1)} %collective-permute-done.14.refs_0_), channel_id=1, source_target_pairs={{0,1},{1,0},{2,3},{3,2},{4,5},{5,4},{6,7},{7,6}} | collective-permute-start | bytes 3145736 | tf_op jit(solution)/shard_map/ppermute | solution.py:473
  700.3 28.9 %collective-permute-start.17 = (bf16[512,512]{1,0:T(8,128)(2,1)}, bf16[512,512]{1,0:T(8,128)(2,1)}, u32[]{:S(2)}, u32[]{:S(2)}) collective-permute-start(bf16[512,512]{1,0:T(8,128)(2,1)} %collective-permute-done.15.refs_1_), channel_id=1, source_target_pairs={{0,1},{1,0},{2,3},{3,2},{4,5},{5,4},{6,7},{7,6}} | collective-permute-start | bytes 1572872 | tf_op jit(solution)/shard_map/ppermute | solution.py:473
  715.6 33.2 %collective-permute-start.10 = (bf16[2,128,2048]{2,1,0:T(8,128)(2,1)}, bf16[2,128,2048]{2,1,0:T(8,128)(2,1)S(1)}, u32[]{:S(2)}, u32[]{:S(2)}) collective-permute-start(bf16[2,128,2048]{2,1,0:T(8,128)(2,1)} %collective-permute-done.8.refs_0_), channel_id=1, source_target_pairs={{0,1},{1,0},{2,3},{3,2},{4,5},{5,4},{6,7},{7,6}} | collective-permute-start | bytes 3145736 | tf_op jit(solution)/shard_map/ppermute | solution.py:473
  722.0 34.1 %collective-permute-start.6 = (bf16[2,128,2048]{2,1,0:T(8,128)(2,1)}, bf16[2,128,2048]{2,1,0:T(8,128)(2,1)S(1)}, u32[]{:S(2)}, u32[]{:S(2)}) collective-permute-start(bf16[2,128,2048]{2,1,0:T(8,128)(2,1)} %collective-permute-done.4.refs_0_), channel_id=1, source_target_pairs={{0,1},{1,0},{2,3},{3,2},{4,5},{5,4},{6,7},{7,6}} | collective-permute-start | bytes 3145736 | tf_op jit(solution)/shard_map/ppermute | solution.py:473
  728.9 19.3 %collective-permute-start = (bf16[2,128,1024]{2,1,0:T(8,128)(2,1)S(1)}, bf16[2,128,1024]{2,1,0:T(8,128)(2,1)S(1)}, u32[]{:S(2)}, u32[]{:S(2)}) collective-permute-start(bf16[2,128,1024]{2,1,0:T(8,128)(2,1)S(1)} %copy-done.11), channel_id=1, source_target_pairs={{0,2},{2,0},{1,3},{3,1},{4,6},{6,4},{5,7},{7,5}} | collective-permute-start | bytes 1572872 | tf_op jit(solution)/shard_map/ppermute | solution.py:477
  729.2 19.1 %collective-permute-start.11 = (bf16[512,512]{1,0:T(8,128)(2,1)}, bf16[512,512]{1,0:T(8,128)(2,1)}, u32[]{:S(2)}, u32[]{:S(2)}) collective-permute-start(bf16[512,512]{1,0:T(8,128)(2,1)} %copy-done.15), channel_id=1, source_target_pairs={{0,1},{1,0},{2,3},{3,2},{4,5},{5,4},{6,7},{7,6}} | collective-permute-start | bytes 1572872 | tf_op jit(solution)/shard_map/ppermute | solution.py:473
  735.7 20.4 %collective-permute-start.7 = (bf16[512,512]{1,0:T(8,128)(2,1)S(1)}, bf16[512,512]{1,0:T(8,128)(2,1)}, u32[]{:S(2)}, u32[]{:S(2)}) collective-permute-start(bf16[512,512]{1,0:T(8,128)(2,1)S(1)} %copy-done.14), channel_id=1, source_target_pairs={{0,1},{1,0},{2,3},{3,2},{4,5},{5,4},{6,7},{7,6}} | collective-permute-start | bytes 1572872 | tf_op jit(solution)/shard_map/ppermute | solution.py:473
  748.2 18.6 %collective-permute-start.3 = (bf16[256,512]{1,0:T(8,128)(2,1)S(1)}, bf16[256,512]{1,0:T(8,128)(2,1)}, u32[]{:S(2)}, u32[]{:S(2)}) collective-permute-start(bf16[256,512]{1,0:T(8,128)(2,1)S(1)} %copy-done.34), channel_id=1, source_target_pairs={{0,1},{1,0},{2,3},{3,2},{4,5},{5,4},{6,7},{7,6}} | collective-permute-start | bytes 786440 | tf_op jit(solution)/shard_map/ppermute | solution.py:473
  748.3 18.5 %collective-permute-start.1 = (bf16[2,128,1024]{2,1,0:T(8,128)(2,1)S(1)}, bf16[2,128,1024]{2,1,0:T(8,128)(2,1)S(1)}, u32[]{:S(2)}, u32[]{:S(2)}) collective-permute-start(bf16[2,128,1024]{2,1,0:T(8,128)(2,1)S(1)} %collective-permute-done.refs_0_), channel_id=1, source_target_pairs={{0,1},{1,0},{2,3},{3,2},{4,5},{5,4},{6,7},{7,6}} | collective-permute-start | bytes 1572872 | tf_op jit(solution)/shard_map/ppermute | solution.py:473
  (44 other events, 1205.2 us)

commit v2 on v1

--- a/solution.py
+++ b/solution.py
@@ -59,7 +59,7 @@
 FT, FI = 1024, 2048
 
 
-def forward_kernel(x_ref, dy_ref, wg_ref, wu_ref, wd_ref, h1_ref, a0_ref, a1_ref, a0t_ref, a1t_ref, dyt_ref, acc_ref, z_ref):
+def forward_kernel(x_ref, wg_ref, wu_ref, wd_ref, h1_ref, a0_ref, a1_ref, a0t_ref, a1t_ref, acc_ref, z_ref):
     j, i = pl.program_id(0), pl.program_id(1)
     rows = pl.ds(pl.multiple_of(i * FI, FI), FI)
 
@@ -68,7 +68,6 @@
         a = normed(x_ref[rows, :])
         a0_ref[rows, :] = a
         a0t_ref[:, rows] = flipped(a)
-        dyt_ref[:, rows] = flipped(dy_ref[rows, :])
         acc_ref[rows, :] = jnp.zeros((FI, D), F32)
 
     a = a0_ref[rows, :]
@@ -87,32 +86,31 @@
         a1t_ref[:, rows] = flipped(a1)
 
 
-def forward(x, dy, wg, wu, wd):
+def forward(x, wg, wu, wd):
     row, col = jax.ShapeDtypeStruct((TOKENS, D), BF16), jax.ShapeDtypeStruct((D, TOKENS), BF16)
     return pl.pallas_call(
         forward_kernel,
         grid=(FF // FT, TOKENS // FI),
         in_specs=[
             whole((TOKENS, D)),
-            whole((TOKENS, D)),
             pl.BlockSpec((1, D, FT), lambda j, i: (0, 0, j)),
             pl.BlockSpec((1, D, FT), lambda j, i: (0, 0, j)),
             pl.BlockSpec((1, FT, D), lambda j, i: (0, j, 0)),
         ],
-        out_specs=[whole((TOKENS, D))] * 3 + [whole((D, TOKENS))] * 3,
-        out_shape=[row] * 3 + [col] * 3,
+        out_specs=[whole((TOKENS, D))] * 3 + [whole((D, TOKENS))] * 2,
+        out_shape=[row] * 3 + [col] * 2,
         scratch_shapes=[pltpu.VMEM((TOKENS, D), F32), pltpu.VMEM((FI, FT), BF16)],
         compiler_params=params(2),
         cost_estimate=cost(3, 40e6),
         name="forward0",
-    )(x, dy, wg, wu, wd)
+    )(x, wg, wu, wd)
 
 
 BI = 512
 
 
 def backward_kernel(
-    h1, a0, a0t, a1, a1t, dy0, dy0t, wg, wu, wd, gu_out, d_out, squares,
+    h1, a0, a0t, a1, a1t, dy0, wg, wu, wd, gu_out, d_out, squares,
     a, at, dy, dyt, h, da, wgu_buf, wd_buf, z, dgu, dt, grads,
     own_gu, far_gu, give_gu, core_gu, x_gu, own_d, far_d, give_d, core_d, x_d, sq,
     w_sem, in_sem, core_send, core_recv, x_send, x_recv, out_sem, sq_send, sq_recv, core_free, x_free,
@@ -142,7 +140,7 @@
         )
 
     def inputs(*sources):
-        pairs = zip(sources, (a, at, dy, dyt, h))
+        pairs = zip(sources, (a, at, dy, h))
         return [pltpu.make_async_copy(src, dst, in_sem.at[n]) for n, (src, dst) in enumerate(pairs)]
 
     def columns_of(half):
@@ -223,12 +221,15 @@
         barrier = pltpu.get_barrier_semaphore()
         for peer in (core_peer, x_peer):
             pl.semaphore_signal(barrier, inc=1, device_id=peer, device_id_type=mesh_id)
-        for copy in (*weights(t), *inputs(a1, a1t, dy0, dy0t, h1)):
+        for copy in (*weights(t), *inputs(a1, a1t, dy0, h1)):
             copy.start()
         da[...] = jnp.zeros_like(da)
         sq[...] = jnp.zeros_like(sq)
-        for copy in inputs(a1, a1t, dy0, dy0t, h1):
+        for copy in inputs(a1, a1t, dy0, h1):
             copy.wait()
+        for b in range(0, TOKENS, BI):
+            rows = slice(b, b + BI)
+            dyt[:, rows] = flipped(dy[rows, :])
         pl.semaphore_wait(barrier, 2)
 
     for copy in weights(t):
@@ -335,7 +336,7 @@
                 copy.wait()
 
 
-def backward(h1, a0, a0t, a1, a1t, dy, dyt, wg, wu, wd):
+def backward(h1, a0, a0t, a1, a1t, dy, wg, wu, wd):
     wide = DP * SIZE
     row, col, vm, dma = (TOKENS, D), (D, TOKENS), pltpu.VMEM, pltpu.SemaphoreType.DMA
     gu, d = (SLOTS, 2, ROWS, wide), (SLOTS, SIZE, D)
@@ -343,7 +344,7 @@
     return pl.pallas_call(
         backward_kernel,
         grid=(STEPS,),
-        in_specs=[pl.BlockSpec(memory_space=pl.ANY)] * 10,
+        in_specs=[pl.BlockSpec(memory_space=pl.ANY)] * 9,
         out_specs=[pl.BlockSpec(memory_space=pl.ANY)] * 2 + [pl.BlockSpec((8, D), lambda t: (0, 0))],
         out_shape=[
             jax.ShapeDtypeStruct((LAYERS * PARTS, 2, ROWS, wide), BF16),
@@ -370,7 +371,7 @@
         ),
         cost_estimate=cost(14, 120e6),
         name="backward",
-    )(h1, a0, a0t, a1, a1t, dy, dyt, wg, wu, wd)
+    )(h1, a0, a0t, a1, a1t, dy, wg, wu, wd)
 
 
 def adamw_kernel(me_ref, f_ref, ggu, gd, wg, wu, wd, mg, mu, md, vg, vu, vd, *refs):
@@ -483,9 +484,9 @@
         x, dy = x[0], dy[0]
         me = lax.axis_index("dp").astype(jnp.int32)[None]
 
-        h1, a0, a1, a0t, a1t, dyt = forward(x, dy, *weights)
-
-        gu, d, squares = backward(h1, a0, a0t, a1, a1t, dy, dyt, *weights)
+        h1, a0, a1, a0t, a1t = forward(x, *weights)
+
+        gu, d, squares = backward(h1, a0, a0t, a1, a1t, dy, *weights)
         d = d.reshape(-1, D)
 
         moments, own, near, far, last, new = (), {}, {}, {}, {}, ()

time: 773 us -> 772 us (level)
  no operation moved by 1% of the time
where the time goes in v2:
time: 772 us; the launch traced here: 769 us
  Pallas kernels  567 us (73%)
  waiting for transfers between devices  175 us (23%)
  starting transfers between devices  14.6 us (2%)
  local copies, waits for them, and re-layouts  11.7 us (2%)
    pallas_call x1, Pallas kernels, backward(): pl.pallas_call(backward_kernel, grid=(STEPS,), in_specs=[pl.BlockSpec(mem...  322 us
    ppermute x18, waiting for transfers between devices, to_x(): return lax.ppermute(t, 'dp', [(0, 2), (2, 0), (1, 3), (3, 1)])  174 us
    pallas_call x19, Pallas kernels, assemble(): pl.pallas_call(functools.partial(assemble_kernel, len(blocks)), grid_spec...  113 us
    pallas_call x9, Pallas kernels, adamw(): pl.pallas_call(adamw_kernel, grid_spec=pltpu.PrefetchScalarGridSpec(num_s...  67 us
    pallas_call x1, Pallas kernels, forward(): pl.pallas_call(forward_kernel, grid=(FF // FT, TOKENS // FI), in_specs=[w...  64.6 us
  transfers between devices with their start and end apart: 54, of which 18 were waited for; matrix products, arithmetic and copies ran while one was open for 0% of the time, Pallas kernels for 22%

profile of v2, /device:TPU:0, one launch (start us, length us, event | category | flops | bytes accessed | tf_op | source)
XLA Modules:
  0.0 768.9 jit_solution(13392007985815473320)
XLA Ops:
  0.6 64.6 %forward0.1 = (bf16[2048,512]{1,0:T(8,128)(2,1)}, bf16[2048,512]{1,0:T(8,128)(2,1)}, bf16[2048,512]{1,0:T(8,128)(2,1)}, bf16[512,2048]{1,0:T(8,128)(2,1)}, bf16[512,2048]{1,0:T(8,128)(2,1)}) custom-call(bf16[2048,512]{1,0:T(8,128)(2,1)} %bitcast.13, bf16[2,512,8192]{2,1,0:T(8,128)(2,1)} %wg.19, bf16[2,512,8192]{2,1,0:T(8,128)(2,1)} %wu.19, ...), custom_call_target="tpu_custom_call" | custom-call | flops 51539607552 | bytes 40000000 | tf_op jit(solution)/shard_map/forward0/pallas_call | solution.py:91
  65.2 322.1 %backward.1 = (bf16[16,2,128,1024]{3,2,1,0:T(8,128)(2,1)}, bf16[16,256,512]{2,1,0:T(8,128)(2,1)}, f32[8,512]{1,0:T(8,128)}) custom-call(bf16[2048,512]{1,0:T(8,128)(2,1)} %get-tuple-element.146.h1, bf16[2048,512]{1,0:T(8,128)(2,1)} %get-tuple-element.147.a0, bf16[512,2048]{1,0:T(8,128)(2,1)} %get-tuple-element.148.a0t, ...), custom_call_target="tpu_custom_call" | custom-call | flops 240518168576 | bytes 120000000 | tf_op jit(solution)/shard_map/backward/pallas_call | solution.py:344
  387.3 5.3 adamw.9
  392.7 2.3 collective-permute-start.45
  395.0 7.9 %adamw.10 = (bf16[2,128,2048]{2,1,0:T(8,128)(2,1)}, bf16[512,512]{1,0:T(8,128)(2,1)}, f32[2,128,8192]{2,1,0:T(8,128)}, f32[2,128,8192]{2,1,0:T(8,128)}, f32[2,20...) custom-call(s32[1]{0:T(128)} %bitcast.me_ref, ...), custom_call_target="tpu_custom_call", output_to_operand_aliasing={{2}: (13, {}), {3}: (14, {}), {4}: (15, {}), {5}: (16, {}),... | custom-call | flops 4294967296 | bytes 17000000 | tf_op jit(solution)/shard_map/adamw/pallas_call | solution.py:409
  402.9 7.9 %adamw.11 = (bf16[2,128,2048]{2,1,0:T(8,128)(2,1)}, bf16[512,512]{1,0:T(8,128)(2,1)}, f32[2,128,8192]{2,1,0:T(8,128)}, f32[2,128,8192]{2,1,0:T(8,128)}, f32[2,20...) custom-call(s32[1]{0:T(128)} %bitcast.me_ref, ...), custom_call_target="tpu_custom_call", output_to_operand_aliasing={{2}: (13, {}), {3}: (14, {}), {4}: (15, {}), {5}: (16, {}),... | custom-call | flops 4294967296 | bytes 17000000 | tf_op jit(solution)/shard_map/adamw/pallas_call | solution.py:409
  410.8 7.9 %adamw.12 = (bf16[2,128,2048]{2,1,0:T(8,128)(2,1)}, bf16[512,512]{1,0:T(8,128)(2,1)}, f32[2,128,8192]{2,1,0:T(8,128)}, f32[2,128,8192]{2,1,0:T(8,128)}, f32[2,20...) custom-call(s32[1]{0:T(128)} %bitcast.me_ref, ...), custom_call_target="tpu_custom_call", output_to_operand_aliasing={{2}: (13, {}), {3}: (14, {}), {4}: (15, {}), {5}: (16, {}),... | custom-call | flops 4294967296 | bytes 17000000 | tf_op jit(solution)/shard_map/adamw/pallas_call | solution.py:409
  418.8 7.9 %adamw.13 = (bf16[2,128,2048]{2,1,0:T(8,128)(2,1)}, bf16[512,512]{1,0:T(8,128)(2,1)}, f32[2,128,8192]{2,1,0:T(8,128)}, f32[2,128,8192]{2,1,0:T(8,128)}, f32[2,20...) custom-call(s32[1]{0:T(128)} %bitcast.me_ref, ...), custom_call_target="tpu_custom_call", output_to_operand_aliasing={{2}: (13, {}), {3}: (14, {}), {4}: (15, {}), {5}: (16, {}),... | custom-call | flops 4294967296 | bytes 17000000 | tf_op jit(solution)/shard_map/adamw/pallas_call | solution.py:409
  426.7 8.0 %adamw.14 = (bf16[2,128,2048]{2,1,0:T(8,128)(2,1)}, bf16[512,512]{1,0:T(8,128)(2,1)}, f32[2,128,8192]{2,1,0:T(8,128)}, f32[2,128,8192]{2,1,0:T(8,128)}, f32[2,20...) custom-call(s32[1]{0:T(128)} %bitcast.me_ref, ...), custom_call_target="tpu_custom_call", output_to_operand_aliasing={{2}: (13, {}), {3}: (14, {}), {4}: (15, {}), {5}: (16, {}),... | custom-call | flops 4294967296 | bytes 17000000 | tf_op jit(solution)/shard_map/adamw/pallas_call | solution.py:409
  434.8 8.1 %adamw.15 = (bf16[2,128,2048]{2,1,0:T(8,128)(2,1)}, bf16[512,512]{1,0:T(8,128)(2,1)}, f32[2,128,8192]{2,1,0:T(8,128)}, f32[2,128,8192]{2,1,0:T(8,128)}, f32[2,20...) custom-call(s32[1]{0:T(128)} %bitcast.me_ref, ...), custom_call_target="tpu_custom_call", output_to_operand_aliasing={{2}: (13, {}), {3}: (14, {}), {4}: (15, {}), {5}: (16, {}),... | custom-call | flops 4294967296 | bytes 17000000 | tf_op jit(solution)/shard_map/adamw/pallas_call | solution.py:409
  442.9 8.1 %adamw.16 = (bf16[2,128,2048]{2,1,0:T(8,128)(2,1)}, bf16[512,512]{1,0:T(8,128)(2,1)}, f32[2,128,8192]{2,1,0:T(8,128)}, f32[2,128,8192]{2,1,0:T(8,128)}, f32[2,20...) custom-call(s32[1]{0:T(128)} %bitcast.me_ref, ...), custom_call_target="tpu_custom_call", output_to_operand_aliasing={{2}: (13, {}), {3}: (14, {}), {4}: (15, {}), {5}: (16, {}),... | custom-call | flops 4294967296 | bytes 17000000 | tf_op jit(solution)/shard_map/adamw/pallas_call | solution.py:409
  451.1 5.6 adamw.17
  459.8 7.4 collective-permute-done.2.refs_1_
  469.4 9.0 %collective-permute-done.44.refs_0_ = bf16[2,128,1024]{2,1,0:T(8,128)(2,1)S(1)} collective-permute-done((bf16[2,128,1024]{2,1,0:T(8,128)(2,1)}, bf16[2,128,1024]{2,1,0:T(8,128)(2,1)S(1)}, u32[]{:S(2)}, u32[]{:S(2)}) %collective-permute-start.44) | collective-permute-done | bytes 524320 | tf_op jit(solution)/shard_map/ppermute | solution.py:478
  478.5 2.0 collective-permute-start.27
  480.5 9.1 %collective-permute-done.39.refs_1_ = bf16[512,512]{1,0:T(8,128)(2,1)S(1)} collective-permute-done((bf16[512,512]{1,0:T(8,128)(2,1)}, bf16[512,512]{1,0:T(8,128)(2,1)S(1)}, u32[]{:S(2)}, u32[]{:S(2)}) %collective-permute-start.39) | collective-permute-done | bytes 524320 | tf_op jit(solution)/shard_map/ppermute | solution.py:478
  489.7 11.1 %collective-permute-done.33.refs_1_ = bf16[512,512]{1,0:T(8,128)(2,1)S(1)} collective-permute-done((bf16[512,512]{1,0:T(8,128)(2,1)}, bf16[512,512]{1,0:T(8,128)(2,1)S(1)}, u32[]{:S(2)}, u32[]{:S(2)}) %collective-permute-start.33) | collective-permute-done | bytes 524320 | tf_op jit(solution)/shard_map/ppermute | solution.py:478
  501.0 11.2 %collective-permute-done.27.refs_1_ = bf16[512,512]{1,0:T(8,128)(2,1)} collective-permute-done((bf16[512,512]{1,0:T(8,128)(2,1)}, bf16[512,512]{1,0:T(8,128)(2,1)}, u32[]{:S(2)}, u32[]{:S(2)}) %collective-permute-start.27) | collective-permute-done | bytes 524320 | tf_op jit(solution)/shard_map/ppermute | solution.py:478
  513.5 9.8 %collective-permute-done.21.refs_1_ = bf16[512,512]{1,0:T(8,128)(2,1)S(1)} collective-permute-done((bf16[512,512]{1,0:T(8,128)(2,1)}, bf16[512,512]{1,0:T(8,128)(2,1)S(1)}, u32[]{:S(2)}, u32[]{:S(2)}) %collective-permute-start.21) | collective-permute-done | bytes 524320 | tf_op jit(solution)/shard_map/ppermute | solution.py:478
  524.1 10.5 %collective-permute-done.15.refs_1_ = bf16[512,512]{1,0:T(8,128)(2,1)} collective-permute-done((bf16[512,512]{1,0:T(8,128)(2,1)}, bf16[512,512]{1,0:T(8,128)(2,1)}, u32[]{:S(2)}, u32[]{:S(2)}) %collective-permute-start.15) | collective-permute-done | bytes 524320 | tf_op jit(solution)/shard_map/ppermute | solution.py:478
  535.5 10.3 %collective-permute-done.9.refs_1_ = bf16[512,512]{1,0:T(8,128)(2,1)S(1)} collective-permute-done((bf16[512,512]{1,0:T(8,128)(2,1)}, bf16[512,512]{1,0:T(8,128)(2,1)S(1)}, u32[]{:S(2)}, u32[]{:S(2)}) %collective-permute-start.9) | collective-permute-done | bytes 524320 | tf_op jit(solution)/shard_map/ppermute | solution.py:478
  545.8 11.2 %collective-permute-done.5.refs_1_ = bf16[512,512]{1,0:T(8,128)(2,1)S(1)} collective-permute-done((bf16[512,512]{1,0:T(8,128)(2,1)S(1)}, bf16[512,512]{1,0:T(8,128)(2,1)S(1)}, u32[]{:S(2)}, u32[]{:S(2)}) %collective-permute-start.5) | collective-permute-done | bytes 524320 | tf_op jit(solution)/shard_map/ppermute | solution.py:478
  560.5 19.1 %collective-permute-done.38.refs_0_ = bf16[2,128,2048]{2,1,0:T(8,128)(2,1)} collective-permute-done((bf16[2,128,2048]{2,1,0:T(8,128)(2,1)}, bf16[2,128,2048]{2,1,0:T(8,128)(2,1)}, u32[]{:S(2)}, u32[]{:S(2)}) %collective-permute-start.38) | collective-permute-done | bytes 1048608 | tf_op jit(solution)/shard_map/ppermute | solution.py:478
  580.2 21.8 %collective-permute-done.32.refs_0_ = bf16[2,128,2048]{2,1,0:T(8,128)(2,1)S(1)} collective-permute-done((bf16[2,128,2048]{2,1,0:T(8,128)(2,1)}, bf16[2,128,2048]{2,1,0:T(8,128)(2,1)S(1)}, u32[]{:S(2)}, u32[]{:S(2)}) %collective-permute-start.32) | collective-permute-done | bytes 1048608 | tf_op jit(solution)/shard_map/ppermute | solution.py:478
  604.2 5.6 assemble.19
  609.8 14.8 %collective-permute-done.26.refs_0_ = bf16[2,128,2048]{2,1,0:T(8,128)(2,1)} collective-permute-done((bf16[2,128,2048]{2,1,0:T(8,128)(2,1)}, bf16[2,128,2048]{2,1,0:T(8,128)(2,1)}, u32[]{:S(2)}, u32[]{:S(2)}) %collective-permute-start.26) | collective-permute-done | bytes 1048608 | tf_op jit(solution)/shard_map/ppermute | solution.py:478
  624.6 6.4 assemble.20
  631.5 6.4 assemble.21
  637.9 9.1 %collective-permute-done.20.refs_0_ = bf16[2,128,2048]{2,1,0:T(8,128)(2,1)} collective-permute-done((bf16[2,128,2048]{2,1,0:T(8,128)(2,1)S(1)}, bf16[2,128,2048]{2,1,0:T(8,128)(2,1)}, u32[]{:S(2)}, u32[]{:S(2)}) %collective-permute-start.20) | collective-permute-done | bytes 1048608 | tf_op jit(solution)/shard_map/ppermute | solution.py:478
  647.1 5.5 assemble.22
  652.7 6.5 assemble.23
  659.2 2.0 collective-permute-start.4
  661.2 6.4 assemble.24
  669.5 6.4 assemble.25
  676.4 6.4 assemble.26
  682.8 9.2 %collective-permute-done.8.refs_0_ = bf16[2,128,2048]{2,1,0:T(8,128)(2,1)} collective-permute-done((bf16[2,128,2048]{2,1,0:T(8,128)(2,1)S(1)}, bf16[2,128,2048]{2,1,0:T(8,128)(2,1)}, u32[]{:S(2)}, u32[]{:S(2)}) %collective-permute-start.8) | collective-permute-done | bytes 1048608 | tf_op jit(solution)/shard_map/ppermute | solution.py:478
  692.0 6.4 assemble.27
  698.9 6.4 assemble.28
  705.2 8.4 %collective-permute-done.4.refs_0_ = bf16[2,128,2048]{2,1,0:T(8,128)(2,1)} collective-permute-done((bf16[2,128,2048]{2,1,0:T(8,128)(2,1)S(1)}, bf16[2,128,2048]{2,1,0:T(8,128)(2,1)}, u32[]{:S(2)}, u32[]{:S(2)}) %collective-permute-start.4) | collective-permute-done | bytes 1048608 | tf_op jit(solution)/shard_map/ppermute | solution.py:478
  713.7 6.4 assemble.29
  720.6 6.4 assemble.30
  727.3 6.5 assemble.31
  734.3 6.4 assemble.32
  740.7 5.6 assemble.33
  747.9 6.4 assemble.34
  755.3 6.4 assemble.35
  761.7 3.2 assemble.36
  765.7 3.2 assemble.37
  (166 shorter events, 22.8 us)
Async XLA Ops:
  392.6 64.8 %collective-permute-start.53 = (bf16[256,512]{1,0:T(8,128)(2,1)}, bf16[256,512]{1,0:T(8,128)(2,1)}, u32[]{:S(2)}, u32[]{:S(2)}) collective-permute-start(bf16[256,512]{1,0:T(8,128)(2,1)} %get-tuple-element.219.refs_1_), channel_id=1, source_target_pairs={{0,1},{1,0},{2,3},{3,2},{4,5},{5,4},{6,7},{7,6}} | collective-permute-start | bytes 786440 | tf_op jit(solution)/shard_map/ppermute | solution.py:474
  392.7 65.1 %collective-permute-start.45 = (bf16[256,512]{1,0:T(8,128)(2,1)}, bf16[256,512]{1,0:T(8,128)(2,1)}, u32[]{:S(2)}, u32[]{:S(2)}) collective-permute-start(bf16[256,512]{1,0:T(8,128)(2,1)} %get-tuple-element.219.refs_1_), channel_id=1, source_target_pairs={{0,2},{2,0},{1,3},{3,1},{4,6},{6,4},{5,7},{7,5}} | collective-permute-start | bytes 786440 | tf_op jit(solution)/shard_map/ppermute | solution.py:478
  457.2 11.2 %collective-permute-start.51 = (bf16[512,512]{1,0:T(8,128)(2,1)}, bf16[512,512]{1,0:T(8,128)(2,1)S(1)}, u32[]{:S(2)}, u32[]{:S(2)}) collective-permute-start(bf16[512,512]{1,0:T(8,128)(2,1)} %get-tuple-element.217.refs_1_), channel_id=1, source_target_pairs={{0,1},{1,0},{2,3},{3,2},{4,5},{5,4},{6,7},{7,6}} | collective-permute-start | bytes 1572872 | tf_op jit(solution)/shard_map/ppermute | solution.py:474
  457.4 11.0 %collective-permute-start.49 = (bf16[512,512]{1,0:T(8,128)(2,1)}, bf16[512,512]{1,0:T(8,128)(2,1)S(1)}, u32[]{:S(2)}, u32[]{:S(2)}) collective-permute-start(bf16[512,512]{1,0:T(8,128)(2,1)} %get-tuple-element.215.refs_1_), channel_id=1, source_target_pairs={{0,1},{1,0},{2,3},{3,2},{4,5},{5,4},{6,7},{7,6}} | collective-permute-start | bytes 1572872 | tf_op jit(solution)/shard_map/ppermute | solution.py:474
  458.5 19.9 %collective-permute-start.44 = (bf16[2,128,1024]{2,1,0:T(8,128)(2,1)}, bf16[2,128,1024]{2,1,0:T(8,128)(2,1)S(1)}, u32[]{:S(2)}, u32[]{:S(2)}) collective-permute-start(bf16[2,128,1024]{2,1,0:T(8,128)(2,1)} %get-tuple-element.218.refs_0_), channel_id=1, source_target_pairs={{0,2},{2,0},{1,3},{3,1},{4,6},{6,4},{5,7},{7,5}} | collective-permute-start | bytes 1572872 | tf_op jit(solution)/shard_map/ppermute | solution.py:478
  468.4 21.2 %collective-permute-start.39 = (bf16[512,512]{1,0:T(8,128)(2,1)}, bf16[512,512]{1,0:T(8,128)(2,1)S(1)}, u32[]{:S(2)}, u32[]{:S(2)}) collective-permute-start(bf16[512,512]{1,0:T(8,128)(2,1)} %get-tuple-element.217.refs_1_), channel_id=1, source_target_pairs={{0,2},{2,0},{1,3},{3,1},{4,6},{6,4},{5,7},{7,5}} | collective-permute-start | bytes 1572872 | tf_op jit(solution)/shard_map/ppermute | solution.py:478
  469.3 20.3 %collective-permute-start.37 = (bf16[512,512]{1,0:T(8,128)(2,1)}, bf16[512,512]{1,0:T(8,128)(2,1)S(1)}, u32[]{:S(2)}, u32[]{:S(2)}) collective-permute-start(bf16[512,512]{1,0:T(8,128)(2,1)} %get-tuple-element.211.refs_1_), channel_id=1, source_target_pairs={{0,1},{1,0},{2,3},{3,2},{4,5},{5,4},{6,7},{7,6}} | collective-permute-start | bytes 1572872 | tf_op jit(solution)/shard_map/ppermute | solution.py:474
  478.4 22.5 %collective-permute-start.33 = (bf16[512,512]{1,0:T(8,128)(2,1)}, bf16[512,512]{1,0:T(8,128)(2,1)S(1)}, u32[]{:S(2)}, u32[]{:S(2)}) collective-permute-start(bf16[512,512]{1,0:T(8,128)(2,1)} %get-tuple-element.215.refs_1_), channel_id=1, source_target_pairs={{0,2},{2,0},{1,3},{3,1},{4,6},{6,4},{5,7},{7,5}} | collective-permute-start | bytes 1572872 | tf_op jit(solution)/shard_map/ppermute | solution.py:478
  478.4 22.5 %collective-permute-start.31 = (bf16[512,512]{1,0:T(8,128)(2,1)}, bf16[512,512]{1,0:T(8,128)(2,1)S(1)}, u32[]{:S(2)}, u32[]{:S(2)}) collective-permute-start(bf16[512,512]{1,0:T(8,128)(2,1)} %get-tuple-element.209.refs_1_), channel_id=1, source_target_pairs={{0,1},{1,0},{2,3},{3,2},{4,5},{5,4},{6,7},{7,6}} | collective-permute-start | bytes 1572872 | tf_op jit(solution)/shard_map/ppermute | solution.py:474
  478.5 33.7 %collective-permute-start.27 = (bf16[512,512]{1,0:T(8,128)(2,1)}, bf16[512,512]{1,0:T(8,128)(2,1)}, u32[]{:S(2)}, u32[]{:S(2)}) collective-permute-start(bf16[512,512]{1,0:T(8,128)(2,1)} %get-tuple-element.213.refs_1_), channel_id=1, source_target_pairs={{0,2},{2,0},{1,3},{3,1},{4,6},{6,4},{5,7},{7,5}} | collective-permute-start | bytes 1572872 | tf_op jit(solution)/shard_map/ppermute | solution.py:478
  489.6 22.6 %collective-permute-start.25 = (bf16[512,512]{1,0:T(8,128)(2,1)}, bf16[512,512]{1,0:T(8,128)(2,1)S(1)}, u32[]{:S(2)}, u32[]{:S(2)}) collective-permute-start(bf16[512,512]{1,0:T(8,128)(2,1)} %get-tuple-element.207.refs_1_), channel_id=1, source_target_pairs={{0,1},{1,0},{2,3},{3,2},{4,5},{5,4},{6,7},{7,6}} | collective-permute-start | bytes 1572872 | tf_op jit(solution)/shard_map/ppermute | solution.py:474
  489.7 33.7 %collective-permute-start.21 = (bf16[512,512]{1,0:T(8,128)(2,1)}, bf16[512,512]{1,0:T(8,128)(2,1)S(1)}, u32[]{:S(2)}, u32[]{:S(2)}) collective-permute-start(bf16[512,512]{1,0:T(8,128)(2,1)} %get-tuple-element.211.refs_1_), channel_id=1, source_target_pairs={{0,2},{2,0},{1,3},{3,1},{4,6},{6,4},{5,7},{7,5}} | collective-permute-start | bytes 1572872 | tf_op jit(solution)/shard_map/ppermute | solution.py:478
  500.9 22.5 %collective-permute-start.19 = (bf16[512,512]{1,0:T(8,128)(2,1)S(1)}, bf16[512,512]{1,0:T(8,128)(2,1)S(1)}, u32[]{:S(2)}, u32[]{:S(2)}) collective-permute-start(bf16[512,512]{1,0:T(8,128)(2,1)S(1)} %copy-done.12), channel_id=1, source_target_pairs={{0,1},{1,0},{2,3},{3,2},{4,5},{5,4},{6,7},{7,6}} | collective-permute-start | bytes 1572872 | tf_op jit(solution)/shard_map/ppermute | solution.py:474
  500.9 33.8 %collective-permute-start.15 = (bf16[512,512]{1,0:T(8,128)(2,1)}, bf16[512,512]{1,0:T(8,128)(2,1)}, u32[]{:S(2)}, u32[]{:S(2)}) collective-permute-start(bf16[512,512]{1,0:T(8,128)(2,1)} %get-tuple-element.209.refs_1_), channel_id=1, source_target_pairs={{0,2},{2,0},{1,3},{3,1},{4,6},{6,4},{5,7},{7,5}} | collective-permute-start | bytes 1572872 | tf_op jit(solution)/shard_map/ppermute | solution.py:478
  512.2 44.8 %collective-permute-start.50 = (bf16[2,128,2048]{2,1,0:T(8,128)(2,1)}, bf16[2,128,2048]{2,1,0:T(8,128)(2,1)S(1)}, u32[]{:S(2)}, u32[]{:S(2)}) collective-permute-start(bf16[2,128,2048]{2,1,0:T(8,128)(2,1)} %get-tuple-element.216.refs_0_), channel_id=1, source_target_pairs={{0,1},{1,0},{2,3},{3,2},{4,5},{5,4},{6,7},{7,6}} | collective-permute-start | bytes 3145736 | tf_op jit(solution)/shard_map/ppermute | solution.py:474
  513.0 21.7 %collective-permute-start.12 = (bf16[2,128,1024]{2,1,0:T(8,128)(2,1)}, bf16[2,128,1024]{2,1,0:T(8,128)(2,1)S(1)}, u32[]{:S(2)}, u32[]{:S(2)}) collective-permute-start(bf16[2,128,1024]{2,1,0:T(8,128)(2,1)} %get-tuple-element.202.refs_0_), channel_id=1, source_target_pairs={{0,1},{1,0},{2,3},{3,2},{4,5},{5,4},{6,7},{7,6}} | collective-permute-start | bytes 1572872 | tf_op jit(solution)/shard_map/ppermute | solution.py:474
  523.3 35.5 %collective-permute-start.48 = (bf16[2,128,2048]{2,1,0:T(8,128)(2,1)}, bf16[2,128,2048]{2,1,0:T(8,128)(2,1)}, u32[]{:S(2)}, u32[]{:S(2)}) collective-permute-start(bf16[2,128,2048]{2,1,0:T(8,128)(2,1)} %get-tuple-element.214.refs_0_), channel_id=1, source_target_pairs={{0,1},{1,0},{2,3},{3,2},{4,5},{5,4},{6,7},{7,6}} | collective-permute-start | bytes 3145736 | tf_op jit(solution)/shard_map/ppermute | solution.py:474
  523.3 22.4 %collective-permute-start.9 = (bf16[512,512]{1,0:T(8,128)(2,1)}, bf16[512,512]{1,0:T(8,128)(2,1)S(1)}, u32[]{:S(2)}, u32[]{:S(2)}) collective-permute-start(bf16[512,512]{1,0:T(8,128)(2,1)} %get-tuple-element.207.refs_1_), channel_id=1, source_target_pairs={{0,2},{2,0},{1,3},{3,1},{4,6},{6,4},{5,7},{7,5}} | collective-permute-start | bytes 1572872 | tf_op jit(solution)/shard_map/ppermute | solution.py:478
  534.7 22.4 %collective-permute-start.5 = (bf16[512,512]{1,0:T(8,128)(2,1)S(1)}, bf16[512,512]{1,0:T(8,128)(2,1)S(1)}, u32[]{:S(2)}, u32[]{:S(2)}) collective-permute-start(bf16[512,512]{1,0:T(8,128)(2,1)S(1)} %copy-done.12), channel_id=1, source_target_pairs={{0,2},{2,0},{1,3},{3,1},{4,6},{6,4},{5,7},{7,5}} | collective-permute-start | bytes 1572872 | tf_op jit(solution)/shard_map/ppermute | solution.py:478
  535.5 23.6 %collective-permute-start.42 = (bf16[2,128,2048]{2,1,0:T(8,128)(2,1)}, bf16[2,128,2048]{2,1,0:T(8,128)(2,1)S(1)}, u32[]{:S(2)}, u32[]{:S(2)}) collective-permute-start(bf16[2,128,2048]{2,1,0:T(8,128)(2,1)} %get-tuple-element.212.refs_0_), channel_id=1, source_target_pairs={{0,1},{1,0},{2,3},{3,2},{4,5},{5,4},{6,7},{7,6}} | collective-permute-start | bytes 3145736 | tf_op jit(solution)/shard_map/ppermute | solution.py:474
  545.8 33.8 %collective-permute-start.38 = (bf16[2,128,2048]{2,1,0:T(8,128)(2,1)}, bf16[2,128,2048]{2,1,0:T(8,128)(2,1)}, u32[]{:S(2)}, u32[]{:S(2)}) collective-permute-start(bf16[2,128,2048]{2,1,0:T(8,128)(2,1)} %get-tuple-element.216.refs_0_), channel_id=1, source_target_pairs={{0,2},{2,0},{1,3},{3,1},{4,6},{6,4},{5,7},{7,5}} | collective-permute-start | bytes 3145736 | tf_op jit(solution)/shard_map/ppermute | solution.py:478
  557.9 21.8 %collective-permute-start.36 = (bf16[2,128,2048]{2,1,0:T(8,128)(2,1)S(1)}, bf16[2,128,2048]{2,1,0:T(8,128)(2,1)S(1)}, u32[]{:S(2)}, u32[]{:S(2)}) collective-permute-start(bf16[2,128,2048]{2,1,0:T(8,128)(2,1)S(1)} %copy-done.3), channel_id=1, source_target_pairs={{0,1},{1,0},{2,3},{3,2},{4,5},{5,4},{6,7},{7,6}} | collective-permute-start | bytes 3145736 | tf_op jit(solution)/shard_map/ppermute | solution.py:474
  558.8 43.1 %collective-permute-start.32 = (bf16[2,128,2048]{2,1,0:T(8,128)(2,1)}, bf16[2,128,2048]{2,1,0:T(8,128)(2,1)S(1)}, u32[]{:S(2)}, u32[]{:S(2)}) collective-permute-start(bf16[2,128,2048]{2,1,0:T(8,128)(2,1)} %get-tuple-element.214.refs_0_), channel_id=1, source_target_pairs={{0,2},{2,0},{1,3},{3,1},{4,6},{6,4},{5,7},{7,5}} | collective-permute-start | bytes 3145736 | tf_op jit(solution)/shard_map/ppermute | solution.py:478
  559.0 20.7 %collective-permute-start.41 = (bf16[512,512]{1,0:T(8,128)(2,1)S(1)}, bf16[512,512]{1,0:T(8,128)(2,1)}, u32[]{:S(2)}, u32[]{:S(2)}) collective-permute-start(bf16[512,512]{1,0:T(8,128)(2,1)S(1)} %collective-permute-done.39.refs_1_), channel_id=1, source_target_pairs={{0,1},{1,0},{2,3},{3,2},{4,5},{5,4},{6,7},{7,6}} | collective-permute-start | bytes 1572872 | tf_op jit(solution)/shard_map/ppermute | solution.py:474
  560.1 41.9 %collective-permute-start.30 = (bf16[2,128,2048]{2,1,0:T(8,128)(2,1)S(1)}, bf16[2,128,2048]{2,1,0:T(8,128)(2,1)S(1)}, u32[]{:S(2)}, u32[]{:S(2)}) collective-permute-start(bf16[2,128,2048]{2,1,0:T(8,128)(2,1)S(1)} %copy-done.2), channel_id=1, source_target_pairs={{0,1},{1,0},{2,3},{3,2},{4,5},{5,4},{6,7},{7,6}} | collective-permute-start | bytes 3145736 | tf_op jit(solution)/shard_map/ppermute | solution.py:474
  579.6 44.9 %collective-permute-start.26 = (bf16[2,128,2048]{2,1,0:T(8,128)(2,1)}, bf16[2,128,2048]{2,1,0:T(8,128)(2,1)}, u32[]{:S(2)}, u32[]{:S(2)}) collective-permute-start(bf16[2,128,2048]{2,1,0:T(8,128)(2,1)} %get-tuple-element.212.refs_0_), channel_id=1, source_target_pairs={{0,2},{2,0},{1,3},{3,1},{4,6},{6,4},{5,7},{7,5}} | collective-permute-start | bytes 3145736 | tf_op jit(solution)/shard_map/ppermute | solution.py:478
  579.7 22.4 %collective-permute-start.35 = (bf16[512,512]{1,0:T(8,128)(2,1)S(1)}, bf16[512,512]{1,0:T(8,128)(2,1)S(1)}, u32[]{:S(2)}, u32[]{:S(2)}) collective-permute-start(bf16[512,512]{1,0:T(8,128)(2,1)S(1)} %collective-permute-done.33.refs_1_), channel_id=1, source_target_pairs={{0,1},{1,0},{2,3},{3,2},{4,5},{5,4},{6,7},{7,6}} | collective-permute-start | bytes 1572872 | tf_op jit(solution)/shard_map/ppermute | solution.py:474
  579.7 51.4 %collective-permute-start.24 = (bf16[2,128,2048]{2,1,0:T(8,128)(2,1)S(1)}, bf16[2,128,2048]{2,1,0:T(8,128)(2,1)}, u32[]{:S(2)}, u32[]{:S(2)}) collective-permute-start(bf16[2,128,2048]{2,1,0:T(8,128)(2,1)S(1)} %copy-done.1), channel_id=1, source_target_pairs={{0,1},{1,0},{2,3},{3,2},{4,5},{5,4},{6,7},{7,6}} | collective-permute-start | bytes 3145736 | tf_op jit(solution)/shard_map/ppermute | solution.py:474
  602.0 45.0 %collective-permute-start.20 = (bf16[2,128,2048]{2,1,0:T(8,128)(2,1)S(1)}, bf16[2,128,2048]{2,1,0:T(8,128)(2,1)}, u32[]{:S(2)}, u32[]{:S(2)}) collective-permute-start(bf16[2,128,2048]{2,1,0:T(8,128)(2,1)S(1)} %copy-done.3), channel_id=1, source_target_pairs={{0,2},{2,0},{1,3},{3,1},{4,6},{6,4},{5,7},{7,5}} | collective-permute-start | bytes 3145736 | tf_op jit(solution)/shard_map/ppermute | solution.py:478
  602.0 22.6 %collective-permute-start.29 = (bf16[512,512]{1,0:T(8,128)(2,1)}, bf16[512,512]{1,0:T(8,128)(2,1)}, u32[]{:S(2)}, u32[]{:S(2)}) collective-permute-start(bf16[512,512]{1,0:T(8,128)(2,1)} %collective-permute-done.27.refs_1_), channel_id=1, source_target_pairs={{0,1},{1,0},{2,3},{3,2},{4,5},{5,4},{6,7},{7,6}} | collective-permute-start | bytes 1572872 | tf_op jit(solution)/shard_map/ppermute | solution.py:474
  604.2 55.0 %collective-permute-start.40 = (bf16[2,128,2048]{2,1,0:T(8,128)(2,1)}, bf16[2,128,2048]{2,1,0:T(8,128)(2,1)}, u32[]{:S(2)}, u32[]{:S(2)}) collective-permute-start(bf16[2,128,2048]{2,1,0:T(8,128)(2,1)} %collective-permute-done.38.refs_0_), channel_id=1, source_target_pairs={{0,1},{1,0},{2,3},{3,2},{4,5},{5,4},{6,7},{7,6}} | collective-permute-start | bytes 3145736 | tf_op jit(solution)/shard_map/ppermute | solution.py:474
  624.6 44.9 %collective-permute-start.14 = (bf16[2,128,2048]{2,1,0:T(8,128)(2,1)S(1)}, bf16[2,128,2048]{2,1,0:T(8,128)(2,1)}, u32[]{:S(2)}, u32[]{:S(2)}) collective-permute-start(bf16[2,128,2048]{2,1,0:T(8,128)(2,1)S(1)} %copy-done.2), channel_id=1, source_target_pairs={{0,2},{2,0},{1,3},{3,1},{4,6},{6,4},{5,7},{7,5}} | collective-permute-start | bytes 3145736 | tf_op jit(solution)/shard_map/ppermute | solution.py:478
  624.6 28.0 %collective-permute-start.23 = (bf16[512,512]{1,0:T(8,128)(2,1)S(1)}, bf16[512,512]{1,0:T(8,128)(2,1)}, u32[]{:S(2)}, u32[]{:S(2)}) collective-permute-start(bf16[512,512]{1,0:T(8,128)(2,1)S(1)} %copy-done.19), channel_id=1, source_target_pairs={{0,1},{1,0},{2,3},{3,2},{4,5},{5,4},{6,7},{7,6}} | collective-permute-start | bytes 1572872 | tf_op jit(solution)/shard_map/ppermute | solution.py:474
  631.1 44.9 %collective-permute-start.34 = (bf16[2,128,2048]{2,1,0:T(8,128)(2,1)}, bf16[2,128,2048]{2,1,0:T(8,128)(2,1)}, u32[]{:S(2)}, u32[]{:S(2)}) collective-permute-start(bf16[2,128,2048]{2,1,0:T(8,128)(2,1)} %copy-done.5), channel_id=1, source_target_pairs={{0,1},{1,0},{2,3},{3,2},{4,5},{5,4},{6,7},{7,6}} | collective-permute-start | bytes 3145736 | tf_op jit(solution)/shard_map/ppermute | solution.py:474
  647.0 44.9 %collective-permute-start.8 = (bf16[2,128,2048]{2,1,0:T(8,128)(2,1)S(1)}, bf16[2,128,2048]{2,1,0:T(8,128)(2,1)}, u32[]{:S(2)}, u32[]{:S(2)}) collective-permute-start(bf16[2,128,2048]{2,1,0:T(8,128)(2,1)S(1)} %copy-done.1), channel_id=1, source_target_pairs={{0,2},{2,0},{1,3},{3,1},{4,6},{6,4},{5,7},{7,5}} | collective-permute-start | bytes 3145736 | tf_op jit(solution)/shard_map/ppermute | solution.py:478
  652.6 45.8 %collective-permute-start.28 = (bf16[2,128,2048]{2,1,0:T(8,128)(2,1)}, bf16[2,128,2048]{2,1,0:T(8,128)(2,1)}, u32[]{:S(2)}, u32[]{:S(2)}) collective-permute-start(bf16[2,128,2048]{2,1,0:T(8,128)(2,1)} %collective-permute-done.26.refs_0_), channel_id=1, source_target_pairs={{0,1},{1,0},{2,3},{3,2},{4,5},{5,4},{6,7},{7,6}} | collective-permute-start | bytes 3145736 | tf_op jit(solution)/shard_map/ppermute | solution.py:474
  659.2 54.5 %collective-permute-start.4 = (bf16[2,128,2048]{2,1,0:T(8,128)(2,1)S(1)}, bf16[2,128,2048]{2,1,0:T(8,128)(2,1)}, u32[]{:S(2)}, u32[]{:S(2)}) collective-permute-start(bf16[2,128,2048]{2,1,0:T(8,128)(2,1)S(1)} %copy-done), channel_id=1, source_target_pairs={{0,2},{2,0},{1,3},{3,1},{4,6},{6,4},{5,7},{7,5}} | collective-permute-start | bytes 3145736 | tf_op jit(solution)/shard_map/ppermute | solution.py:478
  669.5 50.6 %collective-permute-start.22 = (bf16[2,128,2048]{2,1,0:T(8,128)(2,1)}, bf16[2,128,2048]{2,1,0:T(8,128)(2,1)}, u32[]{:S(2)}, u32[]{:S(2)}) collective-permute-start(bf16[2,128,2048]{2,1,0:T(8,128)(2,1)} %collective-permute-done.20.refs_0_), channel_id=1, source_target_pairs={{0,1},{1,0},{2,3},{3,2},{4,5},{5,4},{6,7},{7,6}} | collective-permute-start | bytes 3145736 | tf_op jit(solution)/shard_map/ppermute | solution.py:474
  675.9 51.1 %collective-permute-start.18 = (bf16[2,128,2048]{2,1,0:T(8,128)(2,1)S(1)}, bf16[2,128,2048]{2,1,0:T(8,128)(2,1)}, u32[]{:S(2)}, u32[]{:S(2)}) collective-permute-start(bf16[2,128,2048]{2,1,0:T(8,128)(2,1)S(1)} %copy-done), channel_id=1, source_target_pairs={{0,1},{1,0},{2,3},{3,2},{4,5},{5,4},{6,7},{7,6}} | collective-permute-start | bytes 3145736 | tf_op jit(solution)/shard_map/ppermute | solution.py:474
  692.0 41.8 %collective-permute-start.16 = (bf16[2,128,2048]{2,1,0:T(8,128)(2,1)}, bf16[2,128,2048]{2,1,0:T(8,128)(2,1)}, u32[]{:S(2)}, u32[]{:S(2)}) collective-permute-start(bf16[2,128,2048]{2,1,0:T(8,128)(2,1)} %collective-permute-done.14.refs_0_), channel_id=1, source_target_pairs={{0,1},{1,0},{2,3},{3,2},{4,5},{5,4},{6,7},{7,6}} | collective-permute-start | bytes 3145736 | tf_op jit(solution)/shard_map/ppermute | solution.py:474
  698.4 28.9 %collective-permute-start.17 = (bf16[512,512]{1,0:T(8,128)(2,1)}, bf16[512,512]{1,0:T(8,128)(2,1)}, u32[]{:S(2)}, u32[]{:S(2)}) collective-permute-start(bf16[512,512]{1,0:T(8,128)(2,1)} %collective-permute-done.15.refs_1_), channel_id=1, source_target_pairs={{0,1},{1,0},{2,3},{3,2},{4,5},{5,4},{6,7},{7,6}} | collective-permute-start | bytes 1572872 | tf_op jit(solution)/shard_map/ppermute | solution.py:474
  713.7 33.2 %collective-permute-start.10 = (bf16[2,128,2048]{2,1,0:T(8,128)(2,1)}, bf16[2,128,2048]{2,1,0:T(8,128)(2,1)S(1)}, u32[]{:S(2)}, u32[]{:S(2)}) collective-permute-start(bf16[2,128,2048]{2,1,0:T(8,128)(2,1)} %collective-permute-done.8.refs_0_), channel_id=1, source_target_pairs={{0,1},{1,0},{2,3},{3,2},{4,5},{5,4},{6,7},{7,6}} | collective-permute-start | bytes 3145736 | tf_op jit(solution)/shard_map/ppermute | solution.py:474
  720.1 34.1 %collective-permute-start.6 = (bf16[2,128,2048]{2,1,0:T(8,128)(2,1)}, bf16[2,128,2048]{2,1,0:T(8,128)(2,1)S(1)}, u32[]{:S(2)}, u32[]{:S(2)}) collective-permute-start(bf16[2,128,2048]{2,1,0:T(8,128)(2,1)} %collective-permute-done.4.refs_0_), channel_id=1, source_target_pairs={{0,1},{1,0},{2,3},{3,2},{4,5},{5,4},{6,7},{7,6}} | collective-permute-start | bytes 3145736 | tf_op jit(solution)/shard_map/ppermute | solution.py:474
  727.0 19.3 %collective-permute-start = (bf16[2,128,1024]{2,1,0:T(8,128)(2,1)S(1)}, bf16[2,128,1024]{2,1,0:T(8,128)(2,1)S(1)}, u32[]{:S(2)}, u32[]{:S(2)}) collective-permute-start(bf16[2,128,1024]{2,1,0:T(8,128)(2,1)S(1)} %copy-done.11), channel_id=1, source_target_pairs={{0,2},{2,0},{1,3},{3,1},{4,6},{6,4},{5,7},{7,5}} | collective-permute-start | bytes 1572872 | tf_op jit(solution)/shard_map/ppermute | solution.py:478
  727.3 19.1 %collective-permute-start.11 = (bf16[512,512]{1,0:T(8,128)(2,1)}, bf16[512,512]{1,0:T(8,128)(2,1)}, u32[]{:S(2)}, u32[]{:S(2)}) collective-permute-start(bf16[512,512]{1,0:T(8,128)(2,1)} %copy-done.15), channel_id=1, source_target_pairs={{0,1},{1,0},{2,3},{3,2},{4,5},{5,4},{6,7},{7,6}} | collective-permute-start | bytes 1572872 | tf_op jit(solution)/shard_map/ppermute | solution.py:474
  733.8 20.4 %collective-permute-start.7 = (bf16[512,512]{1,0:T(8,128)(2,1)S(1)}, bf16[512,512]{1,0:T(8,128)(2,1)}, u32[]{:S(2)}, u32[]{:S(2)}) collective-permute-start(bf16[512,512]{1,0:T(8,128)(2,1)S(1)} %copy-done.14), channel_id=1, source_target_pairs={{0,1},{1,0},{2,3},{3,2},{4,5},{5,4},{6,7},{7,6}} | collective-permute-start | bytes 1572872 | tf_op jit(solution)/shard_map/ppermute | solution.py:474
  746.3 18.6 %collective-permute-start.3 = (bf16[256,512]{1,0:T(8,128)(2,1)S(1)}, bf16[256,512]{1,0:T(8,128)(2,1)}, u32[]{:S(2)}, u32[]{:S(2)}) collective-permute-start(bf16[256,512]{1,0:T(8,128)(2,1)S(1)} %copy-done.34), channel_id=1, source_target_pairs={{0,1},{1,0},{2,3},{3,2},{4,5},{5,4},{6,7},{7,6}} | collective-permute-start | bytes 786440 | tf_op jit(solution)/shard_map/ppermute | solution.py:474
  746.4 18.5 %collective-permute-start.1 = (bf16[2,128,1024]{2,1,0:T(8,128)(2,1)S(1)}, bf16[2,128,1024]{2,1,0:T(8,128)(2,1)S(1)}, u32[]{:S(2)}, u32[]{:S(2)}) collective-permute-start(bf16[2,128,1024]{2,1,0:T(8,128)(2,1)S(1)} %collective-permute-done.refs_0_), channel_id=1, source_target_pairs={{0,1},{1,0},{2,3},{3,2},{4,5},{5,4},{6,7},{7,6}} | collective-permute-start | bytes 1572872 | tf_op jit(solution)/shard_map/ppermute | solution.py:474
  (44 other events, 1205.2 us)
